TPU v7x, 32 devices: a whole 2x2x4 slice. The times are simulated.
32 devices in a mesh: blk: 8 (over z, x), shard: 4 (over y, core).
Axes of the slice: x: 2, y: 2, z: 4, core: 2. Of those that a mesh axis runs over, the one named last changes fastest.
Arguments:
- tokens: bfloat16 [8192, 2048], P(('blk', 'shard')), may hold values from -6 to 6
- targets: bfloat16 [8192, 2048], P(('blk', 'shard')), may hold values from -6 to 6
- up_weight: bfloat16 [2048, 7168], P(None, 'shard'), may hold values from -0.125 to 0.125
- down_weight: bfloat16 [8, 7168, 2048], P('blk', 'shard'), may hold values from -6 to 6
- mix_numer: int32 [2, 8, 3], replicated, may hold values from 1 to 2, as said below
Outputs:
- drift: bfloat16 [8, 7168, 2048], P('blk', 'shard')
Inputs may be any that keep to these rules, and one draw needn't show every extreme that they name: Each row of mix_numer is (2, 1, 1), (1, 2, 1) or (1, 1, 2).
All inputs are finite; a program needn't handle non-finite values.
Results may differ from a plain program's by a relative error of at most 0.017.
Values may be sent and summed in bfloat16 or wider, within the bound.
No kernel may reach another device: no remote copies, remote signals or barrier semaphores. Data moves between devices by JAX's collectives and lax.ppermute only.
A program may use at most 128 MiB of HBM per device.

v0:
```python
import functools

import jax
import jax.numpy as jnp
from jax import lax
from jax.experimental import pallas as pl
from jax.experimental.pallas import tpu as pltpu
from jax.sharding import PartitionSpec as P


learn_rate = 2.0
VMEM_LIMIT = 16 * 1024 * 1024
CUTS = (2, 4, 6, 3, 1)


def shifted(x, axis, by):
    devices = lax.axis_size(axis)
    return lax.ppermute(x, axis, [(i, (i + by) % devices) for i in range(devices)])


def exchanged(blocks, sign):
    workers = len(blocks)
    moved = {}
    for j in sorted(range(1, workers), key=lambda j: abs(2 * j - workers)):
        moved[j] = shifted(blocks[j], "blk", sign * j)
    return [blocks[0]] + [moved[j] for j in range(1, workers)]


def other_core(x):
    devices = lax.axis_size("shard")
    return lax.ppermute(x, "shard", [(i, i ^ 1) for i in range(devices)])


def mix_kernel(rounds, workers, weights_ref, *refs):
    mixed = [ref[...].astype(jnp.float32) for ref in refs[:workers]]
    for r in range(rounds):
        mixed = [
            (
                weights_ref[r, j, 0] * mixed[j]
                + weights_ref[r, j, 1] * mixed[(j + 1) % workers]
                + weights_ref[r, j, 2] * mixed[(j - 1) % workers]
            )
            .astype(jnp.bfloat16)
            .astype(jnp.float32)
            for j in range(workers)
        ]
    total = mixed[0]
    for m in mixed[1:]:
        total = total + m
    average = total * (1.0 / workers)
    for j in range(workers):
        refs[workers + j][...] = (mixed[j] - average).astype(jnp.bfloat16)


def mix_blocks(blocks, weights):
    workers = len(blocks)
    rows, width = blocks[0].shape
    tile = next(t for t in (32, 16, 8) if rows % t == 0)
    spec = pl.BlockSpec((tile, width), lambda i: (i, 0))
    return pl.pallas_call(
        functools.partial(mix_kernel, weights.shape[0], workers),
        grid=(rows // tile,),
        in_specs=[pl.BlockSpec(memory_space=pltpu.SMEM)] + [spec] * workers,
        out_specs=[spec] * workers,
        out_shape=[jax.ShapeDtypeStruct((rows, width), jnp.bfloat16)] * workers,
        cost_estimate=pl.CostEstimate(
            flops=20 * workers * rows * width,
            bytes_accessed=4 * workers * rows * width,
            transcendentals=0,
        ),
        compiler_params=pltpu.CompilerParams(vmem_limit_bytes=VMEM_LIMIT // 2),
        name="mix_blocks",
    )(weights, *blocks)


def place_kernel(begin, *refs):
    blocks, result_ref, sems = refs[: -2], refs[-2], refs[-1]
    workers, _, _ = result_ref.shape
    blocks = blocks[:workers]
    me = lax.axis_index("blk")
    copies = []
    for j in range(workers):
        target = result_ref.at[lax.rem(me + j, workers), :, pl.ds(begin, blocks[j].shape[1])]
        copies.append(pltpu.make_async_copy(blocks[j], target, sems.at[j]))
    for copy in copies:
        copy.start()
    for copy in copies:
        copy.wait()


def place_blocks(blocks, begin, shape, result):
    workers = len(blocks)
    inside = pl.BlockSpec(memory_space=pltpu.VMEM)
    outside = pl.BlockSpec(memory_space=pl.ANY)
    held = [] if result is None else [result]
    return pl.pallas_call(
        functools.partial(place_kernel, begin),
        in_specs=[inside] * workers + [outside] * len(held),
        out_specs=outside,
        out_shape=jax.ShapeDtypeStruct(shape, jnp.bfloat16),
        scratch_shapes=[pltpu.SemaphoreType.DMA((workers,))],
        input_output_aliases={workers: 0} if held else {},
        cost_estimate=pl.CostEstimate(
            flops=4 * blocks[0].size * workers, bytes_accessed=4 * blocks[0].size * workers, transcendentals=0
        ),
        compiler_params=pltpu.CompilerParams(vmem_limit_bytes=VMEM_LIMIT // 2),
        name="place_blocks",
    )(*blocks, *held)


def out_kernel(begin, scale, *refs):
    hidden_refs, (targets_ref, weight_ref, own_ref, other_ref, part_ref, sem) = refs[:-6], refs[-6:]
    _, step = own_ref.shape[1:]
    copy = pltpu.make_async_copy(weight_ref.at[:, pl.ds(begin, step)], part_ref, sem)
    copy.start()
    copy.wait()
    for d in range(own_ref.shape[0]):
        own, other = (
            jnp.dot(ref[...], part_ref[...], preferred_element_type=jnp.float32) * scale
            for ref in hidden_refs[2 * d : 2 * d + 2]
        )
        if d == 0:
            own = own - targets_ref[:, begin : begin + step].astype(jnp.float32)
        own_ref[d] = own
        other_ref[d] = other.astype(jnp.bfloat16)


def out_part(hidden, targets, weight, begin, step, scale):
    chips, rows = len(hidden) // 2, targets.shape[0]
    inside = pl.BlockSpec(memory_space=pltpu.VMEM)
    outside = pl.BlockSpec(memory_space=pl.ANY)
    units = weight.shape[0]
    return pl.pallas_call(
        functools.partial(out_kernel, begin, scale),
        in_specs=[inside] * (2 * chips + 1) + [outside],
        out_specs=[inside, inside],
        out_shape=[
            jax.ShapeDtypeStruct((chips, rows, step), jnp.float32),
            jax.ShapeDtypeStruct((chips, rows, step), jnp.bfloat16),
        ],
        scratch_shapes=[pltpu.VMEM((units, step), jnp.bfloat16), pltpu.SemaphoreType.DMA],
        compiler_params=pltpu.CompilerParams(vmem_limit_bytes=VMEM_LIMIT),
        cost_estimate=pl.CostEstimate(
            flops=4 * chips * rows * units * step, bytes_accessed=2 * units * step, transcendentals=0
        ),
        name="out_part",
    )(*hidden, targets, weight)


def grad_kernel(begin, scale, chips, unrolled, *refs):
    hidden_refs, refs = refs[: 2 * chips], refs[2 * chips :]
    resid_ref, other_ref, weight_ref = refs[:3]
    block_refs, (part_ref, stepped_ref, sem) = refs[3:-3], refs[-3:]
    workers = len(block_refs)
    step = resid_ref.shape[2]
    units = part_ref.shape[0]
    block = units // workers
    tile = next(t for t in (256, 128) if units % t == 0)
    copy = pltpu.make_async_copy(weight_ref.at[:, pl.ds(begin, step)], part_ref, sem)
    copy.start()

    def one_tile(i):
        at = pl.ds(i * tile if isinstance(i, int) else pl.multiple_of(i * tile, tile), tile)
        grad = None
        for piece, hidden_ref in enumerate(hidden_refs):
            term = lax.dot_general(
                hidden_ref[:, at],
                (resid_ref, other_ref)[piece % 2][piece // 2],
                (((0,), (0,)), ((), ())),
                preferred_element_type=jnp.float32,
            )
            grad = term if grad is None else grad + term
        pl.when(i == 0)(copy.wait)
        stepped_ref[at] = (part_ref[at].astype(jnp.float32) - scale * grad).astype(jnp.bfloat16)

    if unrolled:
        for i in range(units // tile):
            one_tile(i)
    else:
        pl.loop(0, units // tile)(one_tile)
    me = lax.axis_index("blk")
    for j in range(workers):
        first = pl.multiple_of(lax.rem(me + j, workers) * block, 8)
        block_refs[j][...] = stepped_ref[pl.ds(first, block), :]


def grad_part(hidden, resid, other, weight, begin, scale, workers, unrolled):
    chips, rows, step = resid.shape
    units = weight.shape[0]
    inside = pl.BlockSpec(memory_space=pltpu.VMEM)
    outside = pl.BlockSpec(memory_space=pl.ANY)
    return pl.pallas_call(
        functools.partial(grad_kernel, begin, scale, chips, unrolled),
        in_specs=[inside] * (2 * chips + 2) + [outside],
        out_specs=[inside] * workers,
        out_shape=[jax.ShapeDtypeStruct((units // workers, step), jnp.bfloat16)] * workers,
        scratch_shapes=[
            pltpu.VMEM((units, step), jnp.bfloat16),
            pltpu.VMEM((units, step), jnp.bfloat16),
            pltpu.SemaphoreType.DMA,
        ],
        compiler_params=pltpu.CompilerParams(vmem_limit_bytes=VMEM_LIMIT),
        cost_estimate=pl.CostEstimate(
            flops=4 * chips * rows * units * step, bytes_accessed=4 * units * step, transcendentals=0
        ),
        name="grad_part",
    )(*hidden, resid, other, weight)


def body(tokens, targets, up_weight, down_weight, mix_numer):
    weight = down_weight[0]
    units, width = weight.shape
    workers = lax.axis_size("blk")
    me = lax.axis_index("blk")
    shards = lax.axis_size("shard")
    chips = shards // 2
    block = units // workers
    out_scale = 1.0 / (units * shards) ** 0.5
    parts = len(CUTS)

    mine = [tokens] + [shifted(tokens, "shard", -2 * d) for d in range(1, chips)]
    hidden = []
    for x in mine:
        pair = (x, other_core(x))
        for x in pair:
            hidden.append(jax.nn.silu(jnp.dot(x, up_weight, preferred_element_type=jnp.float32)).astype(jnp.bfloat16))

    order = (me - jnp.arange(workers)) % workers
    weights = jnp.take(mix_numer, order, axis=1).astype(jnp.float32) * 0.25

    unit = width // sum(CUTS)
    begins = [unit * sum(CUTS[:c]) for c in range(parts)]
    arrived = []
    for c in range(parts):
        step = unit * CUTS[c]
        own, other = out_part(hidden, targets, weight, begins[c], step, out_scale)
        summed = (own + other_core(other).astype(jnp.float32)).astype(jnp.bfloat16)
        total = summed.astype(jnp.float32)
        for d in range(1, chips):
            got = shifted(summed, "shard", -2 * d).astype(jnp.float32)
            total = total + jnp.roll(got, d, axis=0)
        resid = total.astype(jnp.bfloat16)
        other = other_core(resid)
        blocks = grad_part(hidden, resid, other, weight, begins[c], learn_rate * out_scale, workers, c < 2)
        arrived.append(exchanged(blocks, 1))
    returned = []
    for c in range(parts):
        drift = mix_blocks(arrived[c], weights)
        returned.append(exchanged(drift, -1))
    result = None
    for c in range(parts):
        result = place_blocks(returned[c], begins[c], (workers, block, width), result)
    return result.reshape(1, units, width)


def solution(mesh):
    in_specs = (P(("blk", "shard"), None), P(("blk", "shard"), None), P(None, "shard"), P("blk", "shard", None), P())

    return jax.shard_map(body, mesh=mesh, in_specs=in_specs, out_specs=P("blk", "shard", None), check_vma=False)
```

profile of v0, /device:TPU:0, one launch (start us, length us, event | category | flops | bytes accessed | tf_op | source)
XLA Modules:
  0.0 422.0 jit_solution(17354426513508876401)
XLA Ops:
  3.0 5.6 %multiply_convert_fusion.3.refs_0_ = bf16[256,1792]{1,0:T(8,128)(2,1)S(1)} fusion(bf16[256,2048]{1,0:T(8,128)(2,1)} %param.5, bf16[2048,1792]{1,0:T(8,128)(2,1)} %param.7), kind=kOutput, calls=%fused_computation.4 | convolution fusion | flops 1881341952 | bytes 9306112 | tf_op jit(solution)/shard_map/dot_general | solution.py:226
  9.4 17.0 %collective-permute-done.1 = bf16[256,2048]{1,0:T(8,128)(2,1)S(1)} collective-permute-done((bf16[256,2048]{1,0:T(8,128)(2,1)}, bf16[256,2048]{1,0:T(8,128)(2,1)S(1)}, u32[]{:S(2)}, u32[]{:S(2)}) %collective-permute-start.1) | collective-permute-done | bytes 1048608 | tf_op jit(solution)/shard_map/ppermute | solution.py:18
  26.4 5.3 %multiply_convert_fusion.1.refs_2_ = bf16[256,1792]{1,0:T(8,128)(2,1)S(1)} fusion(bf16[256,2048]{1,0:T(8,128)(2,1)S(1)} %collective-permute-done.1, bf16[2048,1792]{1,0:T(8,128)(2,1)} %param.7), kind=kOutput, calls=%fused_computation.2 | convolution fusion | flops 1881341952 | bytes 9306112 | tf_op jit(solution)/shard_map/dot_general | solution.py:226
  88.7 4.5 %collective-permute-done.76.refs_3_ = bf16[224,256]{1,0:T(8,128)(2,1)S(1)} collective-permute-done((bf16[224,256]{1,0:T(8,128)(2,1)S(1)}, bf16[224,256]{1,0:T(8,128)(2,1)S(1)}, u32[]{:S(2)}, u32[]{:S(2)}) %collective-permute-start.76) | collective-permute-done | bytes 114720 | tf_op jit(solution)/shard_map/ppermute | solution.py:18
  93.2 6.7 %collective-permute-start.79 = (bf16[224,256]{1,0:T(8,128)(2,1)S(1)}, bf16[224,256]{1,0:T(8,128)(2,1)S(1)}, u32[]{:S(2)}, u32[]{:S(2)}) collective-permute-start(bf16[224,256]{1,0:T(8,128)(2,1)S(1)} %get-tuple-element.175), channel_id=1, source_target_pairs={{0,24},{4,28},{8,0},{12,4},{16,8},{20,12},{24,16},{28,20},{1,25},{... | collective-permute-start | bytes 344072 | tf_op jit(solution)/shard_map/ppermute | solution.py:18
  125.9 16.1 %collective-permute-start.27 = (bf16[224,384]{1,0:T(8,128)(2,1)S(1)}, bf16[224,384]{1,0:T(8,128)(2,1)S(1)}, u32[]{:S(2)}, u32[]{:S(2)}) collective-permute-start(bf16[224,384]{1,0:T(8,128)(2,1)S(1)} %get-tuple-element.120), channel_id=1, source_target_pairs={{0,20},{4,24},{8,28},{12,0},{16,4},{20,8},{24,12},{28,16},{1,21},{... | collective-permute-start | bytes 516104 | tf_op jit(solution)/shard_map/ppermute | solution.py:18
  144.8 6.7 %collective-permute-start.29 = (bf16[224,384]{1,0:T(8,128)(2,1)S(1)}, bf16[224,384]{1,0:T(8,128)(2,1)S(1)}, u32[]{:S(2)}, u32[]{:S(2)}) collective-permute-start(bf16[224,384]{1,0:T(8,128)(2,1)S(1)} %get-tuple-element.122), channel_id=1, source_target_pairs={{0,28},{4,0},{8,4},{12,8},{16,12},{20,16},{24,20},{28,24},{1,29},{... | collective-permute-start | bytes 516104 | tf_op jit(solution)/shard_map/ppermute | solution.py:18
  154.9 8.1 %collective-permute-start.85 = (bf16[224,256]{1,0:T(8,128)(2,1)S(1)}, bf16[224,256]{1,0:T(8,128)(2,1)S(1)}, u32[]{:S(2)}, u32[]{:S(2)}) collective-permute-start(bf16[224,256]{1,0:T(8,128)(2,1)S(1)} %get-tuple-element.182), channel_id=1, source_target_pairs={{0,12},{4,16},{8,20},{12,24},{16,28},{20,0},{24,4},{28,8},{1,13},{... | collective-permute-start | bytes 344072 | tf_op jit(solution)/shard_map/ppermute | solution.py:18
  167.6 6.7 %collective-permute-done.86.refs_6_ = bf16[224,256]{1,0:T(8,128)(2,1)S(1)} collective-permute-done((bf16[224,256]{1,0:T(8,128)(2,1)S(1)}, bf16[224,256]{1,0:T(8,128)(2,1)S(1)}, u32[]{:S(2)}, u32[]{:S(2)}) %collective-permute-start.86) | collective-permute-done | bytes 114720 | tf_op jit(solution)/shard_map/ppermute | solution.py:18
  181.8 12.5 %collective-permute-start.35 = (bf16[224,384]{1,0:T(8,128)(2,1)S(1)}, bf16[224,384]{1,0:T(8,128)(2,1)S(1)}, u32[]{:S(2)}, u32[]{:S(2)}) collective-permute-start(bf16[224,384]{1,0:T(8,128)(2,1)S(1)} %get-tuple-element.129), channel_id=1, source_target_pairs={{0,8},{4,12},{8,16},{12,20},{16,24},{20,28},{24,0},{28,4},{1,9},{5... | collective-permute-start | bytes 516104 | tf_op jit(solution)/shard_map/ppermute | solution.py:18
  197.8 22.9 %collective-permute-done.34.refs_5_ = bf16[224,384]{1,0:T(8,128)(2,1)S(1)} collective-permute-done((bf16[224,384]{1,0:T(8,128)(2,1)S(1)}, bf16[224,384]{1,0:T(8,128)(2,1)S(1)}, u32[]{:S(2)}, u32[]{:S(2)}) %collective-permute-start.34) | collective-permute-done | bytes 172064 | tf_op jit(solution)/shard_map/ppermute | solution.py:18
  221.4 5.6 %grad_part.7 = (bf16[224,768]{1,0:T(8,128)(2,1)S(1)}, bf16[224,768]{1,0:T(8,128)(2,1)S(1)}, bf16[224,768]{1,0:T(8,128)(2,1)S(1)}, bf16[224,768]{1,0:T(8,128)(2,1...) custom-call(bf16[256,1792]{1,0:T(8,128)(2,1)S(1)} %multiply_convert_, ...), custom_call_target="tpu_custom_call" | custom-call | flops 2818572288 | bytes 5505024 | tf_op jit(solution)/shard_map/grad_part/pallas_call | solution.py:192
  232.4 11.3 %collective-permute-done.59.refs_3_ = bf16[224,512]{1,0:T(8,128)(2,1)S(1)} collective-permute-done((bf16[224,512]{1,0:T(8,128)(2,1)S(1)}, bf16[224,512]{1,0:T(8,128)(2,1)S(1)}, u32[]{:S(2)}, u32[]{:S(2)}) %collective-permute-start.59) | collective-permute-done | bytes 229408 | tf_op jit(solution)/shard_map/ppermute | solution.py:18
  249.8 9.4 %collective-permute-start.43 = (bf16[224,768]{1,0:T(8,128)(2,1)S(1)}, bf16[224,768]{1,0:T(8,128)(2,1)S(1)}, u32[]{:S(2)}, u32[]{:S(2)}) collective-permute-start(bf16[224,768]{1,0:T(8,128)(2,1)S(1)} %get-tuple-element.137), channel_id=1, source_target_pairs={{0,16},{4,20},{8,24},{12,28},{16,0},{20,4},{24,8},{28,12},{1,17},{... | collective-permute-start | bytes 1032200 | tf_op jit(solution)/shard_map/ppermute | solution.py:18
  265.4 9.4 %collective-permute-start.45 = (bf16[224,768]{1,0:T(8,128)(2,1)S(1)}, bf16[224,768]{1,0:T(8,128)(2,1)S(1)}, u32[]{:S(2)}, u32[]{:S(2)}) collective-permute-start(bf16[224,768]{1,0:T(8,128)(2,1)S(1)} %get-tuple-element.139), channel_id=1, source_target_pairs={{0,24},{4,28},{8,0},{12,4},{16,8},{20,12},{24,16},{28,20},{1,25},{... | collective-permute-start | bytes 1032200 | tf_op jit(solution)/shard_map/ppermute | solution.py:18
  282.1 6.5 %collective-permute-start.36 = (bf16[224,384]{1,0:T(8,128)(2,1)S(1)}, bf16[224,384]{1,0:T(8,128)(2,1)S(1)}, u32[]{:S(2)}, u32[]{:S(2)}) collective-permute-start(bf16[224,384]{1,0:T(8,128)(2,1)S(1)} %get-tuple-element.130), channel_id=1, source_target_pairs={{0,4},{4,8},{8,12},{12,16},{16,20},{20,24},{24,28},{28,0},{1,5},{5... | collective-permute-start | bytes 516104 | tf_op jit(solution)/shard_map/ppermute | solution.py:18
  288.6 15.6 %collective-permute-start.65 = (bf16[224,512]{1,0:T(8,128)(2,1)S(1)}, bf16[224,512]{1,0:T(8,128)(2,1)S(1)}, u32[]{:S(2)}, u32[]{:S(2)}) collective-permute-start(bf16[224,512]{1,0:T(8,128)(2,1)S(1)} %get-tuple-element.161), channel_id=1, source_target_pairs={{0,24},{4,28},{8,0},{12,4},{16,8},{20,12},{24,16},{28,20},{1,25},{... | collective-permute-start | bytes 688136 | tf_op jit(solution)/shard_map/ppermute | solution.py:18
  305.7 28.9 %collective-permute-start.67 = (bf16[224,512]{1,0:T(8,128)(2,1)S(1)}, bf16[224,512]{1,0:T(8,128)(2,1)S(1)}, u32[]{:S(2)}, u32[]{:S(2)}) collective-permute-start(bf16[224,512]{1,0:T(8,128)(2,1)S(1)} %get-tuple-element.163), channel_id=1, source_target_pairs={{0,16},{4,20},{8,24},{12,28},{16,0},{20,4},{24,8},{28,12},{1,17},{... | collective-permute-start | bytes 688136 | tf_op jit(solution)/shard_map/ppermute | solution.py:18
  342.3 11.3 %collective-permute-start.69 = (bf16[224,512]{1,0:T(8,128)(2,1)S(1)}, bf16[224,512]{1,0:T(8,128)(2,1)S(1)}, u32[]{:S(2)}, u32[]{:S(2)}) collective-permute-start(bf16[224,512]{1,0:T(8,128)(2,1)S(1)} %get-tuple-element.165), channel_id=1, source_target_pairs={{0,8},{4,12},{8,16},{12,20},{16,24},{20,28},{24,0},{28,4},{1,9},{5... | collective-permute-start | bytes 688136 | tf_op jit(solution)/shard_map/ppermute | solution.py:18
  353.6 12.5 %collective-permute-done.67.refs_4_ = bf16[224,512]{1,0:T(8,128)(2,1)S(1)} collective-permute-done((bf16[224,512]{1,0:T(8,128)(2,1)S(1)}, bf16[224,512]{1,0:T(8,128)(2,1)S(1)}, u32[]{:S(2)}, u32[]{:S(2)}) %collective-permute-start.67) | collective-permute-done | bytes 229408 | tf_op jit(solution)/shard_map/ppermute | solution.py:18
  366.2 17.1 %collective-permute-done.68.refs_5_ = bf16[224,512]{1,0:T(8,128)(2,1)S(1)} collective-permute-done((bf16[224,512]{1,0:T(8,128)(2,1)S(1)}, bf16[224,512]{1,0:T(8,128)(2,1)S(1)}, u32[]{:S(2)}, u32[]{:S(2)}) %collective-permute-start.68) | collective-permute-done | bytes 229408 | tf_op jit(solution)/shard_map/ppermute | solution.py:18
  387.8 4.8 %collective-permute-done.49.refs_3_ = bf16[224,768]{1,0:T(8,128)(2,1)S(1)} collective-permute-done((bf16[224,768]{1,0:T(8,128)(2,1)S(1)}, bf16[224,768]{1,0:T(8,128)(2,1)S(1)}, u32[]{:S(2)}, u32[]{:S(2)}) %collective-permute-start.49) | collective-permute-done | bytes 344096 | tf_op jit(solution)/shard_map/ppermute | solution.py:18
  393.7 8.0 %collective-permute-done.50.refs_4_ = bf16[224,768]{1,0:T(8,128)(2,1)S(1)} collective-permute-done((bf16[224,768]{1,0:T(8,128)(2,1)S(1)}, bf16[224,768]{1,0:T(8,128)(2,1)S(1)}, u32[]{:S(2)}, u32[]{:S(2)}) %collective-permute-start.50) | collective-permute-done | bytes 344096 | tf_op jit(solution)/shard_map/ppermute | solution.py:18
  401.8 12.2 %collective-permute-done.51.refs_5_ = bf16[224,768]{1,0:T(8,128)(2,1)S(1)} collective-permute-done((bf16[224,768]{1,0:T(8,128)(2,1)S(1)}, bf16[224,768]{1,0:T(8,128)(2,1)S(1)}, u32[]{:S(2)}, u32[]{:S(2)}) %collective-permute-start.51) | collective-permute-done | bytes 344096 | tf_op jit(solution)/shard_map/ppermute | solution.py:18
  (211 shorter events, 156.4 us)
Async XLA Ops:
  3.0 28.6 %collective-permute-start = (bf16[256,2048]{1,0:T(8,128)(2,1)}, bf16[256,2048]{1,0:T(8,128)(2,1)S(1)}, u32[]{:S(2)}, u32[]{:S(2)}) collective-permute-start(bf16[256,2048]{1,0:T(8,128)(2,1)} %param.5), channel_id=1, source_target_pairs={{0,1},{1,0},{2,3},{3,2},{4,5},{5,4},{6,7},{7,6},{8,9},{9,8},{10,11... | collective-permute-start | bytes 3145736 | tf_op jit(solution)/shard_map/ppermute | solution.py:31
  76.4 32.8 %collective-permute-start.55 = (bf16[2,256,512]{2,1,0:T(8,128)(2,1)S(1)}, bf16[2,256,512]{2,1,0:T(8,128)(2,1)S(1)}, u32[]{:S(2)}, u32[]{:S(2)}) collective-permute-start(bf16[2,256,512]{2,1,0:T(8,128)(2,1)S(1)} %add_convert_fusion.1), channel_id=1, source_target_pairs={{0,2},{1,3},{2,0},{3,1},{4,6},{5,7},{6,4},{7,5},{8,10},{9,11},{10,... | collective-permute-start | bytes 1572872 | tf_op jit(solution)/shard_map/ppermute | solution.py:18
  123.5 97.2 %collective-permute-start.39 = (bf16[2,256,768]{2,1,0:T(8,128)(2,1)S(1)}, bf16[2,256,768]{2,1,0:T(8,128)(2,1)S(1)}, u32[]{:S(2)}, u32[]{:S(2)}) collective-permute-start(bf16[2,256,768]{2,1,0:T(8,128)(2,1)S(1)} %fusion.refs_4_), channel_id=1, source_target_pairs={{0,1},{1,0},{2,3},{3,2},{4,5},{5,4},{6,7},{7,6},{8,9},{9,8},{10,11... | collective-permute-start | bytes 2359304 | tf_op jit(solution)/shard_map/ppermute | solution.py:31
  125.8 50.9 %collective-permute-start.56 = (bf16[2,256,512]{2,1,0:T(8,128)(2,1)S(1)}, bf16[2,256,512]{2,1,0:T(8,128)(2,1)S(1)}, u32[]{:S(2)}, u32[]{:S(2)}) collective-permute-start(bf16[2,256,512]{2,1,0:T(8,128)(2,1)S(1)} %fusion.1.refs_4_), channel_id=1, source_target_pairs={{0,1},{1,0},{2,3},{3,2},{4,5},{5,4},{6,7},{7,6},{8,9},{9,8},{10,11... | collective-permute-start | bytes 1572872 | tf_op jit(solution)/shard_map/ppermute | solution.py:31
  176.7 44.0 %collective-permute-start.34 = (bf16[224,384]{1,0:T(8,128)(2,1)S(1)}, bf16[224,384]{1,0:T(8,128)(2,1)S(1)}, u32[]{:S(2)}, u32[]{:S(2)}) collective-permute-start(bf16[224,384]{1,0:T(8,128)(2,1)S(1)} %get-tuple-element.128), channel_id=1, source_target_pairs={{0,12},{4,16},{8,20},{12,24},{16,28},{20,0},{24,4},{28,8},{1,13},{... | collective-permute-start | bytes 516104 | tf_op jit(solution)/shard_map/ppermute | solution.py:18
  181.8 45.2 %collective-permute-start.35 = (bf16[224,384]{1,0:T(8,128)(2,1)S(1)}, bf16[224,384]{1,0:T(8,128)(2,1)S(1)}, u32[]{:S(2)}, u32[]{:S(2)}) collective-permute-start(bf16[224,384]{1,0:T(8,128)(2,1)S(1)} %get-tuple-element.129), channel_id=1, source_target_pairs={{0,8},{4,12},{8,16},{12,20},{16,24},{20,28},{24,0},{28,4},{1,9},{5... | collective-permute-start | bytes 516104 | tf_op jit(solution)/shard_map/ppermute | solution.py:18
  194.3 36.5 %collective-permute-start.57 = (bf16[224,512]{1,0:T(8,128)(2,1)S(1)}, bf16[224,512]{1,0:T(8,128)(2,1)S(1)}, u32[]{:S(2)}, u32[]{:S(2)}) collective-permute-start(bf16[224,512]{1,0:T(8,128)(2,1)S(1)} %get-tuple-element.152), channel_id=1, source_target_pairs={{0,4},{4,8},{8,12},{12,16},{16,20},{20,24},{24,28},{28,0},{1,5},{5... | collective-permute-start | bytes 688136 | tf_op jit(solution)/shard_map/ppermute | solution.py:18
  197.8 33.0 %collective-permute-start.58 = (bf16[224,512]{1,0:T(8,128)(2,1)S(1)}, bf16[224,512]{1,0:T(8,128)(2,1)S(1)}, u32[]{:S(2)}, u32[]{:S(2)}) collective-permute-start(bf16[224,512]{1,0:T(8,128)(2,1)S(1)} %get-tuple-element.153), channel_id=1, source_target_pairs={{0,8},{4,12},{8,16},{12,20},{16,24},{20,28},{24,0},{28,4},{1,9},{5... | collective-permute-start | bytes 688136 | tf_op jit(solution)/shard_map/ppermute | solution.py:18
  227.0 38.3 %collective-permute-start.40 = (bf16[224,768]{1,0:T(8,128)(2,1)S(1)}, bf16[224,768]{1,0:T(8,128)(2,1)S(1)}, u32[]{:S(2)}, u32[]{:S(2)}) collective-permute-start(bf16[224,768]{1,0:T(8,128)(2,1)S(1)} %get-tuple-element.134), channel_id=1, source_target_pairs={{0,4},{4,8},{8,12},{12,16},{16,20},{20,24},{24,28},{28,0},{1,5},{5... | collective-permute-start | bytes 1032200 | tf_op jit(solution)/shard_map/ppermute | solution.py:18
  230.8 44.0 %collective-permute-start.41 = (bf16[224,768]{1,0:T(8,128)(2,1)S(1)}, bf16[224,768]{1,0:T(8,128)(2,1)S(1)}, u32[]{:S(2)}, u32[]{:S(2)}) collective-permute-start(bf16[224,768]{1,0:T(8,128)(2,1)S(1)} %get-tuple-element.135), channel_id=1, source_target_pairs={{0,8},{4,12},{8,16},{12,20},{16,24},{20,28},{24,0},{28,4},{1,9},{5... | collective-permute-start | bytes 1032200 | tf_op jit(solution)/shard_map/ppermute | solution.py:18
  245.7 35.0 %collective-permute-start.42 = (bf16[224,768]{1,0:T(8,128)(2,1)S(1)}, bf16[224,768]{1,0:T(8,128)(2,1)S(1)}, u32[]{:S(2)}, u32[]{:S(2)}) collective-permute-start(bf16[224,768]{1,0:T(8,128)(2,1)S(1)} %get-tuple-element.136), channel_id=1, source_target_pairs={{0,12},{4,16},{8,20},{12,24},{16,28},{20,0},{24,4},{28,8},{1,13},{... | collective-permute-start | bytes 1032200 | tf_op jit(solution)/shard_map/ppermute | solution.py:18
  249.8 32.3 %collective-permute-start.43 = (bf16[224,768]{1,0:T(8,128)(2,1)S(1)}, bf16[224,768]{1,0:T(8,128)(2,1)S(1)}, u32[]{:S(2)}, u32[]{:S(2)}) collective-permute-start(bf16[224,768]{1,0:T(8,128)(2,1)S(1)} %get-tuple-element.137), channel_id=1, source_target_pairs={{0,16},{4,20},{8,24},{12,28},{16,0},{20,4},{24,8},{28,12},{1,17},{... | collective-permute-start | bytes 1032200 | tf_op jit(solution)/shard_map/ppermute | solution.py:18
  265.4 38.8 %collective-permute-start.45 = (bf16[224,768]{1,0:T(8,128)(2,1)S(1)}, bf16[224,768]{1,0:T(8,128)(2,1)S(1)}, u32[]{:S(2)}, u32[]{:S(2)}) collective-permute-start(bf16[224,768]{1,0:T(8,128)(2,1)S(1)} %get-tuple-element.139), channel_id=1, source_target_pairs={{0,24},{4,28},{8,0},{12,4},{16,8},{20,12},{24,16},{28,20},{1,25},{... | collective-permute-start | bytes 1032200 | tf_op jit(solution)/shard_map/ppermute | solution.py:18
  274.8 30.8 %collective-permute-start.46 = (bf16[224,768]{1,0:T(8,128)(2,1)S(1)}, bf16[224,768]{1,0:T(8,128)(2,1)S(1)}, u32[]{:S(2)}, u32[]{:S(2)}) collective-permute-start(bf16[224,768]{1,0:T(8,128)(2,1)S(1)} %get-tuple-element.140), channel_id=1, source_target_pairs={{0,28},{4,0},{8,4},{12,8},{16,12},{20,16},{24,20},{28,24},{1,29},{... | collective-permute-start | bytes 1032200 | tf_op jit(solution)/shard_map/ppermute | solution.py:18
  280.7 58.2 %collective-permute-start.64 = (bf16[224,512]{1,0:T(8,128)(2,1)S(1)}, bf16[224,512]{1,0:T(8,128)(2,1)S(1)}, u32[]{:S(2)}, u32[]{:S(2)}) collective-permute-start(bf16[224,512]{1,0:T(8,128)(2,1)S(1)} %get-tuple-element.160), channel_id=1, source_target_pairs={{0,28},{4,0},{8,4},{12,8},{16,12},{20,16},{24,20},{28,24},{1,29},{... | collective-permute-start | bytes 688136 | tf_op jit(solution)/shard_map/ppermute | solution.py:18
  282.1 56.7 %collective-permute-start.36 = (bf16[224,384]{1,0:T(8,128)(2,1)S(1)}, bf16[224,384]{1,0:T(8,128)(2,1)S(1)}, u32[]{:S(2)}, u32[]{:S(2)}) collective-permute-start(bf16[224,384]{1,0:T(8,128)(2,1)S(1)} %get-tuple-element.130), channel_id=1, source_target_pairs={{0,4},{4,8},{8,12},{12,16},{16,20},{20,24},{24,28},{28,0},{1,5},{5... | collective-permute-start | bytes 516104 | tf_op jit(solution)/shard_map/ppermute | solution.py:18
  288.6 51.8 %collective-permute-start.65 = (bf16[224,512]{1,0:T(8,128)(2,1)S(1)}, bf16[224,512]{1,0:T(8,128)(2,1)S(1)}, u32[]{:S(2)}, u32[]{:S(2)}) collective-permute-start(bf16[224,512]{1,0:T(8,128)(2,1)S(1)} %get-tuple-element.161), channel_id=1, source_target_pairs={{0,24},{4,28},{8,0},{12,4},{16,8},{20,12},{24,16},{28,20},{1,25},{... | collective-permute-start | bytes 688136 | tf_op jit(solution)/shard_map/ppermute | solution.py:18
  304.1 38.2 %collective-permute-start.66 = (bf16[224,512]{1,0:T(8,128)(2,1)S(1)}, bf16[224,512]{1,0:T(8,128)(2,1)S(1)}, u32[]{:S(2)}, u32[]{:S(2)}) collective-permute-start(bf16[224,512]{1,0:T(8,128)(2,1)S(1)} %get-tuple-element.162), channel_id=1, source_target_pairs={{0,20},{4,24},{8,28},{12,0},{16,4},{20,8},{24,12},{28,16},{1,21},{... | collective-permute-start | bytes 688136 | tf_op jit(solution)/shard_map/ppermute | solution.py:18
  305.7 60.5 %collective-permute-start.67 = (bf16[224,512]{1,0:T(8,128)(2,1)S(1)}, bf16[224,512]{1,0:T(8,128)(2,1)S(1)}, u32[]{:S(2)}, u32[]{:S(2)}) collective-permute-start(bf16[224,512]{1,0:T(8,128)(2,1)S(1)} %get-tuple-element.163), channel_id=1, source_target_pairs={{0,16},{4,20},{8,24},{12,28},{16,0},{20,4},{24,8},{28,12},{1,17},{... | collective-permute-start | bytes 688136 | tf_op jit(solution)/shard_map/ppermute | solution.py:18
  338.8 47.5 %collective-permute-start.47 = (bf16[224,768]{1,0:T(8,128)(2,1)S(1)}, bf16[224,768]{1,0:T(8,128)(2,1)S(1)}, u32[]{:S(2)}, u32[]{:S(2)}) collective-permute-start(bf16[224,768]{1,0:T(8,128)(2,1)S(1)} %get-tuple-element.142), channel_id=1, source_target_pairs={{0,28},{4,0},{8,4},{12,8},{16,12},{20,16},{24,20},{28,24},{1,29},{... | collective-permute-start | bytes 1032200 | tf_op jit(solution)/shard_map/ppermute | solution.py:18
  338.9 47.4 %collective-permute-start.48 = (bf16[224,768]{1,0:T(8,128)(2,1)S(1)}, bf16[224,768]{1,0:T(8,128)(2,1)S(1)}, u32[]{:S(2)}, u32[]{:S(2)}) collective-permute-start(bf16[224,768]{1,0:T(8,128)(2,1)S(1)} %get-tuple-element.143), channel_id=1, source_target_pairs={{0,24},{4,28},{8,0},{12,4},{16,8},{20,12},{24,16},{28,20},{1,25},{... | collective-permute-start | bytes 1032200 | tf_op jit(solution)/shard_map/ppermute | solution.py:18
  340.4 42.9 %collective-permute-start.68 = (bf16[224,512]{1,0:T(8,128)(2,1)S(1)}, bf16[224,512]{1,0:T(8,128)(2,1)S(1)}, u32[]{:S(2)}, u32[]{:S(2)}) collective-permute-start(bf16[224,512]{1,0:T(8,128)(2,1)S(1)} %get-tuple-element.164), channel_id=1, source_target_pairs={{0,12},{4,16},{8,20},{12,24},{16,28},{20,0},{24,4},{28,8},{1,13},{... | collective-permute-start | bytes 688136 | tf_op jit(solution)/shard_map/ppermute | solution.py:18
  342.3 41.0 %collective-permute-start.69 = (bf16[224,512]{1,0:T(8,128)(2,1)S(1)}, bf16[224,512]{1,0:T(8,128)(2,1)S(1)}, u32[]{:S(2)}, u32[]{:S(2)}) collective-permute-start(bf16[224,512]{1,0:T(8,128)(2,1)S(1)} %get-tuple-element.165), channel_id=1, source_target_pairs={{0,8},{4,12},{8,16},{12,20},{16,24},{20,28},{24,0},{28,4},{1,9},{5... | collective-permute-start | bytes 688136 | tf_op jit(solution)/shard_map/ppermute | solution.py:18
  383.3 30.7 %collective-permute-start.51 = (bf16[224,768]{1,0:T(8,128)(2,1)S(1)}, bf16[224,768]{1,0:T(8,128)(2,1)S(1)}, u32[]{:S(2)}, u32[]{:S(2)}) collective-permute-start(bf16[224,768]{1,0:T(8,128)(2,1)S(1)} %get-tuple-element.146), channel_id=1, source_target_pairs={{0,12},{4,16},{8,20},{12,24},{16,28},{20,0},{24,4},{28,8},{1,13},{... | collective-permute-start | bytes 1032200 | tf_op jit(solution)/shard_map/ppermute | solution.py:18
  (70 other events, 921.9 us)
where the time goes:
time: 422 us
  starting transfers between devices  210 us (50%)
  waiting for transfers between devices  147 us (35%)
  Pallas kernels  46.6 us (11%)
  matrix products  15.2 us (4%)
    ppermute x76, starting transfers between devices, shifted(): lax.ppermute(x, axis, [(i, (i + by) % devices) for i in range(devices)])  208 us
    ppermute x76, waiting for transfers between devices, shifted(): lax.ppermute(x, axis, [(i, (i + by) % devices) for i in range(devices)])  146 us
    pallas_call x5, Pallas kernels, grad_part(): pl.pallas_call(functools.partial(grad_kernel, begin, scale, chips, unroll...  16.8 us
    dot_general x4, matrix products, body(): jnp.dot(x, up_weight, preferred_element_type=jnp.float32)  15.2 us
    pallas_call x5, Pallas kernels, mix_blocks(): pl.pallas_call(functools.partial(mix_kernel, weights.shape[0], workers),...  13.1 us
    pallas_call x5, Pallas kernels, out_part(): pl.pallas_call(functools.partial(out_kernel, begin, scale), in_specs=[ins...  10.8 us
  transfers between devices with their start and end apart: 88, of which 29 were waited for; matrix products, arithmetic and copies ran while one was open for 4% of the time, Pallas kernels for 9%

commit v1 on v0

--- a/solution.py
+++ b/solution.py
@@ -9,8 +9,9 @@
 
 
 learn_rate = 2.0
+AHEAD = 3
 VMEM_LIMIT = 16 * 1024 * 1024
-CUTS = (2, 4, 6, 3, 1)
+CUTS = (2, 4, 5, 3, 2)
 
 
 def shifted(x, axis, by):
@@ -109,30 +110,32 @@
 
 
 def out_kernel(begin, scale, *refs):
-    hidden_refs, (targets_ref, weight_ref, own_ref, other_ref, part_ref, sem) = refs[:-6], refs[-6:]
-    _, step = own_ref.shape[1:]
+    weight_ref, own_ref, other_ref, part_ref, sem = refs[-5:]
+    chips = own_ref.shape[0]
+    hidden_refs, targets_refs = refs[: 2 * chips], refs[2 * chips : -5]
+    step = own_ref.shape[2]
     copy = pltpu.make_async_copy(weight_ref.at[:, pl.ds(begin, step)], part_ref, sem)
     copy.start()
     copy.wait()
-    for d in range(own_ref.shape[0]):
+    for d in range(chips):
         own, other = (
             jnp.dot(ref[...], part_ref[...], preferred_element_type=jnp.float32) * scale
             for ref in hidden_refs[2 * d : 2 * d + 2]
         )
-        if d == 0:
-            own = own - targets_ref[:, begin : begin + step].astype(jnp.float32)
+        if d == 0 and targets_refs:
+            own = own - targets_refs[0][:, begin : begin + step].astype(jnp.float32)
         own_ref[d] = own
         other_ref[d] = other.astype(jnp.bfloat16)
 
 
 def out_part(hidden, targets, weight, begin, step, scale):
-    chips, rows = len(hidden) // 2, targets.shape[0]
+    chips, rows = len(hidden) // 2, hidden[0].shape[0]
     inside = pl.BlockSpec(memory_space=pltpu.VMEM)
     outside = pl.BlockSpec(memory_space=pl.ANY)
     units = weight.shape[0]
     return pl.pallas_call(
         functools.partial(out_kernel, begin, scale),
-        in_specs=[inside] * (2 * chips + 1) + [outside],
+        in_specs=[inside] * (2 * chips + len(targets)) + [outside],
         out_specs=[inside, inside],
         out_shape=[
             jax.ShapeDtypeStruct((chips, rows, step), jnp.float32),
@@ -144,7 +147,7 @@
             flops=4 * chips * rows * units * step, bytes_accessed=2 * units * step, transcendentals=0
         ),
         name="out_part",
-    )(*hidden, targets, weight)
+    )(*hidden, *targets, weight)
 
 
 def grad_kernel(begin, scale, chips, unrolled, *refs):
@@ -233,13 +236,34 @@
     arrived = []
     for c in range(parts):
         step = unit * CUTS[c]
-        own, other = out_part(hidden, targets, weight, begins[c], step, out_scale)
-        summed = (own + other_core(other).astype(jnp.float32)).astype(jnp.bfloat16)
-        total = summed.astype(jnp.float32)
-        for d in range(1, chips):
-            got = shifted(summed, "shard", -2 * d).astype(jnp.float32)
-            total = total + jnp.roll(got, d, axis=0)
-        resid = total.astype(jnp.bfloat16)
+        runs = ((0, 1), (1, chips)) if c < AHEAD and chips > 1 else ((0, chips),)
+        sums = []
+        got = {}
+        for first, last in runs:
+            own, other = out_part(
+                hidden[2 * first : 2 * last],
+                [] if first else [targets],
+                weight,
+                begins[c],
+                step,
+                out_scale,
+            )
+            if sums:
+                own, *sums = lax.optimization_barrier((own, *sums))
+            summed = (own + other_core(other).astype(jnp.float32)).astype(jnp.bfloat16)
+            sums += [summed[i] for i in range(last - first)]
+            if c and last < chips:
+                continue
+            sent = summed if c == 0 or len(runs) == 1 else jnp.stack(sums)
+            for d in range(1, chips):
+                moved = shifted(sent, "shard", -2 * d)
+                for i in range(sent.shape[0]):
+                    got.setdefault((d + i + (first if c == 0 else 0)) % chips, []).append(moved[i])
+        totals = [x.astype(jnp.float32) for x in sums]
+        for n, terms in got.items():
+            for x in terms:
+                totals[n] = totals[n] + x.astype(jnp.float32)
+        resid = jnp.stack(totals).astype(jnp.bfloat16)
         other = other_core(resid)
         blocks = grad_part(hidden, resid, other, weight, begins[c], learn_rate * out_scale, workers, c < 2)
         arrived.append(exchanged(blocks, 1))

time: 422 us -> 429 us (1.017)
  waiting for transfers between devices: 147 us -> 160 us
  starting transfers between devices: 210 us -> 205 us
    ppermute x76 -> x77, waiting for transfers between devices: 146 us -> 160 us  [shifted(): lax.ppermute(x, axis, [(i, (i + by) % devices) for i in range(devices)])]
    ppermute x76 -> x77, starting transfers between devices: 208 us -> 202 us  [shifted(): lax.ppermute(x, axis, [(i, (i + by) % devices) for i in range(devices)])]
    pallas_call x5 -> x8, Pallas kernels: 10.8 us -> 12.1 us  [out_part(): pl.pallas_call(functools.partial(out_kernel, begin, scale), in_specs=[ins...]
  transfers between devices with their start and end apart: 88 -> 92, of which waited for: 29 -> 28; matrix products, arithmetic and copies ran while one was open for 4% -> 4% of each run, Pallas kernels for 9% -> 11%
where the time goes in v1:
time: 429 us
  starting transfers between devices  205 us (48%)
  waiting for transfers between devices  160 us (37%)
  Pallas kernels  47.8 us (11%)
  matrix products  12.4 us (3%)
    ppermute x77, starting transfers between devices, shifted(): lax.ppermute(x, axis, [(i, (i + by) % devices) for i in range(devices)])  202 us
    ppermute x77, waiting for transfers between devices, shifted(): lax.ppermute(x, axis, [(i, (i + by) % devices) for i in range(devices)])  160 us
    pallas_call x5, Pallas kernels, grad_part(): pl.pallas_call(functools.partial(grad_kernel, begin, scale, chips, unroll...  16.7 us
    pallas_call x5, Pallas kernels, mix_blocks(): pl.pallas_call(functools.partial(mix_kernel, weights.shape[0], workers),...  13.1 us
    dot_general x4, matrix products, body(): jnp.dot(x, up_weight, preferred_element_type=jnp.float32)  12.4 us
    pallas_call x8, Pallas kernels, out_part(): pl.pallas_call(functools.partial(out_kernel, begin, scale), in_specs=[ins...  12.1 us
  transfers between devices with their start and end apart: 92, of which 28 were waited for; matrix products, arithmetic and copies ran while one was open for 4% of the time, Pallas kernels for 11%

profile of v1, /device:TPU:0, one launch (start us, length us, event | category | flops | bytes accessed | tf_op | source)
XLA Modules:
  0.0 429.2 jit_solution(13809873963485709917)
XLA Ops:
  4.4 5.7 %multiply_convert_fusion.3.refs_0_ = bf16[256,1792]{1,0:T(8,128)(2,1)S(1)} fusion(bf16[256,2048]{1,0:T(8,128)(2,1)} %param.5, bf16[2048,1792]{1,0:T(8,128)(2,1)} %param.7), kind=kOutput, calls=%fused_computation.4 | convolution fusion | flops 1881341952 | bytes 9306112 | tf_op jit(solution)/shard_map/dot_general | solution.py:229
  17.8 9.3 %collective-permute-done.1 = bf16[256,2048]{1,0:T(8,128)(2,1)S(1)} collective-permute-done((bf16[256,2048]{1,0:T(8,128)(2,1)}, bf16[256,2048]{1,0:T(8,128)(2,1)S(1)}, u32[]{:S(2)}, u32[]{:S(2)}) %collective-permute-start.1) | collective-permute-done | bytes 1048608 | tf_op jit(solution)/shard_map/ppermute | solution.py:19
  50.1 5.0 %collective-permute-done.4 = bf16[2,256,256]{2,1,0:T(8,128)(2,1)S(1)} collective-permute-done((bf16[2,256,256]{2,1,0:T(8,128)(2,1)S(1)}, bf16[2,256,256]{2,1,0:T(8,128)(2,1)S(1)}, u32[]{:S(2)}, u32[]{:S(2)}) %collective-permute-start.4) | collective-permute-done | bytes 262176 | tf_op jit(solution)/shard_map/ppermute | solution.py:19
  67.2 6.2 %collective-permute-done.80.refs_3_ = bf16[224,256]{1,0:T(8,128)(2,1)S(1)} collective-permute-done((bf16[224,256]{1,0:T(8,128)(2,1)S(1)}, bf16[224,256]{1,0:T(8,128)(2,1)S(1)}, u32[]{:S(2)}, u32[]{:S(2)}) %collective-permute-start.80) | collective-permute-done | bytes 114720 | tf_op jit(solution)/shard_map/ppermute | solution.py:19
  85.2 5.1 %collective-permute-start.85 = (bf16[224,256]{1,0:T(8,128)(2,1)S(1)}, bf16[224,256]{1,0:T(8,128)(2,1)S(1)}, u32[]{:S(2)}, u32[]{:S(2)}) collective-permute-start(bf16[224,256]{1,0:T(8,128)(2,1)S(1)} %get-tuple-element.202), channel_id=1, source_target_pairs={{0,28},{4,0},{8,4},{12,8},{16,12},{20,16},{24,20},{28,24},{1,29},{... | collective-permute-start | bytes 344072 | tf_op jit(solution)/shard_map/ppermute | solution.py:19
  93.8 7.5 %collective-permute-done.39 = bf16[2,256,640]{2,1,0:T(8,128)(2,1)S(1)} collective-permute-done((bf16[2,256,640]{2,1,0:T(8,128)(2,1)S(1)}, bf16[2,256,640]{2,1,0:T(8,128)(2,1)S(1)}, u32[]{:S(2)}, u32[]{:S(2)}) %collective-permute-start.39) | collective-permute-done | bytes 655392 | tf_op jit(solution)/shard_map/ppermute | solution.py:19
  123.0 8.4 %collective-permute-start.25 = (bf16[224,384]{1,0:T(8,128)(2,1)S(1)}, bf16[224,384]{1,0:T(8,128)(2,1)S(1)}, u32[]{:S(2)}, u32[]{:S(2)}) collective-permute-start(bf16[224,384]{1,0:T(8,128)(2,1)S(1)} %get-tuple-element.130), channel_id=1, source_target_pairs={{0,12},{4,16},{8,20},{12,24},{16,28},{20,0},{24,4},{28,8},{1,13},{... | collective-permute-start | bytes 516104 | tf_op jit(solution)/shard_map/ppermute | solution.py:19
  131.4 12.0 %collective-permute-done.8.refs_3_ = bf16[224,256]{1,0:T(8,128)(2,1)S(1)} collective-permute-done((bf16[224,256]{1,0:T(8,128)(2,1)S(1)}, bf16[224,256]{1,0:T(8,128)(2,1)S(1)}, u32[]{:S(2)}, u32[]{:S(2)}) %collective-permute-start.8) | collective-permute-done | bytes 114720 | tf_op jit(solution)/shard_map/ppermute | solution.py:19
  147.1 4.6 %collective-permute-done.26.refs_4_ = bf16[224,384]{1,0:T(8,128)(2,1)S(1)} collective-permute-done((bf16[224,384]{1,0:T(8,128)(2,1)S(1)}, bf16[224,384]{1,0:T(8,128)(2,1)S(1)}, u32[]{:S(2)}, u32[]{:S(2)}) %collective-permute-start.26) | collective-permute-done | bytes 172064 | tf_op jit(solution)/shard_map/ppermute | solution.py:19
  151.6 8.3 %collective-permute-start.29 = (bf16[224,384]{1,0:T(8,128)(2,1)S(1)}, bf16[224,384]{1,0:T(8,128)(2,1)S(1)}, u32[]{:S(2)}, u32[]{:S(2)}) collective-permute-start(bf16[224,384]{1,0:T(8,128)(2,1)S(1)} %get-tuple-element.134), channel_id=1, source_target_pairs={{0,28},{4,0},{8,4},{12,8},{16,12},{20,16},{24,20},{28,24},{1,29},{... | collective-permute-start | bytes 516104 | tf_op jit(solution)/shard_map/ppermute | solution.py:19
  192.4 12.5 %collective-permute-start.60 = (bf16[224,512]{1,0:T(8,128)(2,1)S(1)}, bf16[224,512]{1,0:T(8,128)(2,1)S(1)}, u32[]{:S(2)}, u32[]{:S(2)}) collective-permute-start(bf16[224,512]{1,0:T(8,128)(2,1)S(1)} %get-tuple-element.173), channel_id=1, source_target_pairs={{0,8},{4,12},{8,16},{12,20},{16,24},{20,28},{24,0},{28,4},{1,9},{5... | collective-permute-start | bytes 688136 | tf_op jit(solution)/shard_map/ppermute | solution.py:19
  204.9 15.6 %collective-permute-done.33.refs_4_ = bf16[224,384]{1,0:T(8,128)(2,1)S(1)} collective-permute-done((bf16[224,384]{1,0:T(8,128)(2,1)S(1)}, bf16[224,384]{1,0:T(8,128)(2,1)S(1)}, u32[]{:S(2)}, u32[]{:S(2)}) %collective-permute-start.33) | collective-permute-done | bytes 172064 | tf_op jit(solution)/shard_map/ppermute | solution.py:19
  220.5 12.6 %collective-permute-done.34.refs_5_ = bf16[224,384]{1,0:T(8,128)(2,1)S(1)} collective-permute-done((bf16[224,384]{1,0:T(8,128)(2,1)S(1)}, bf16[224,384]{1,0:T(8,128)(2,1)S(1)}, u32[]{:S(2)}, u32[]{:S(2)}) %collective-permute-start.34) | collective-permute-done | bytes 172064 | tf_op jit(solution)/shard_map/ppermute | solution.py:19
  233.2 5.4 %grad_part.7 = (bf16[224,640]{1,0:T(8,128)(2,1)S(1)}, bf16[224,640]{1,0:T(8,128)(2,1)S(1)}, bf16[224,640]{1,0:T(8,128)(2,1)S(1)}, bf16[224,640]{1,0:T(8,128)(2,1...) custom-call(bf16[256,1792]{1,0:T(8,128)(2,1)S(1)} %multiply_convert_, ...), custom_call_target="tpu_custom_call" | custom-call | flops 2348810240 | bytes 4587520 | tf_op jit(solution)/shard_map/grad_part/pallas_call | solution.py:195
  248.1 6.1 %collective-permute-start.64 = (bf16[224,512]{1,0:T(8,128)(2,1)S(1)}, bf16[224,512]{1,0:T(8,128)(2,1)S(1)}, u32[]{:S(2)}, u32[]{:S(2)}) collective-permute-start(bf16[224,512]{1,0:T(8,128)(2,1)S(1)} %get-tuple-element.177), channel_id=1, source_target_pairs={{0,24},{4,28},{8,0},{12,4},{16,8},{20,12},{24,16},{28,20},{1,25},{... | collective-permute-start | bytes 688136 | tf_op jit(solution)/shard_map/ppermute | solution.py:19
  254.7 5.0 %collective-permute-done.63.refs_5_ = bf16[224,512]{1,0:T(8,128)(2,1)S(1)} collective-permute-done((bf16[224,512]{1,0:T(8,128)(2,1)S(1)}, bf16[224,512]{1,0:T(8,128)(2,1)S(1)}, u32[]{:S(2)}, u32[]{:S(2)}) %collective-permute-start.63) | collective-permute-done | bytes 229408 | tf_op jit(solution)/shard_map/ppermute | solution.py:19
  261.8 27.5 %collective-permute-start.44 = (bf16[224,640]{1,0:T(8,128)(2,1)S(1)}, bf16[224,640]{1,0:T(8,128)(2,1)S(1)}, u32[]{:S(2)}, u32[]{:S(2)}) collective-permute-start(bf16[224,640]{1,0:T(8,128)(2,1)S(1)} %get-tuple-element.153), channel_id=1, source_target_pairs={{0,16},{4,20},{8,24},{12,28},{16,0},{20,4},{24,8},{28,12},{1,17},{... | collective-permute-start | bytes 860168 | tf_op jit(solution)/shard_map/ppermute | solution.py:19
  299.2 5.3 %collective-permute-done.44.refs_4_ = bf16[224,640]{1,0:T(8,128)(2,1)S(1)} collective-permute-done((bf16[224,640]{1,0:T(8,128)(2,1)S(1)}, bf16[224,640]{1,0:T(8,128)(2,1)S(1)}, u32[]{:S(2)}, u32[]{:S(2)}) %collective-permute-start.44) | collective-permute-done | bytes 286752 | tf_op jit(solution)/shard_map/ppermute | solution.py:19
  304.6 16.4 %collective-permute-start.67 = (bf16[224,512]{1,0:T(8,128)(2,1)S(1)}, bf16[224,512]{1,0:T(8,128)(2,1)S(1)}, u32[]{:S(2)}, u32[]{:S(2)}) collective-permute-start(bf16[224,512]{1,0:T(8,128)(2,1)S(1)} %get-tuple-element.181), channel_id=1, source_target_pairs={{0,24},{4,28},{8,0},{12,4},{16,8},{20,12},{24,16},{28,20},{1,25},{... | collective-permute-start | bytes 688136 | tf_op jit(solution)/shard_map/ppermute | solution.py:19
  328.9 7.4 %collective-permute-done.36.refs_7_ = bf16[224,384]{1,0:T(8,128)(2,1)S(1)} collective-permute-done((bf16[224,384]{1,0:T(8,128)(2,1)S(1)}, bf16[224,384]{1,0:T(8,128)(2,1)S(1)}, u32[]{:S(2)}, u32[]{:S(2)}) %collective-permute-start.36) | collective-permute-done | bytes 172064 | tf_op jit(solution)/shard_map/ppermute | solution.py:19
  350.3 17.4 %collective-permute-done.70.refs_5_ = bf16[224,512]{1,0:T(8,128)(2,1)S(1)} collective-permute-done((bf16[224,512]{1,0:T(8,128)(2,1)S(1)}, bf16[224,512]{1,0:T(8,128)(2,1)S(1)}, u32[]{:S(2)}, u32[]{:S(2)}) %collective-permute-start.70) | collective-permute-done | bytes 229408 | tf_op jit(solution)/shard_map/ppermute | solution.py:19
  367.7 10.6 %collective-permute-start.52 = (bf16[224,640]{1,0:T(8,128)(2,1)S(1)}, bf16[224,640]{1,0:T(8,128)(2,1)S(1)}, u32[]{:S(2)}, u32[]{:S(2)}) collective-permute-start(bf16[224,640]{1,0:T(8,128)(2,1)S(1)} %get-tuple-element.162), channel_id=1, source_target_pairs={{0,12},{4,16},{8,20},{12,24},{16,28},{20,0},{24,4},{28,8},{1,13},{... | collective-permute-start | bytes 860168 | tf_op jit(solution)/shard_map/ppermute | solution.py:19
  381.7 19.6 %collective-permute-start.15 = (bf16[224,256]{1,0:T(8,128)(2,1)S(1)}, bf16[224,256]{1,0:T(8,128)(2,1)S(1)}, u32[]{:S(2)}, u32[]{:S(2)}) collective-permute-start(bf16[224,256]{1,0:T(8,128)(2,1)S(1)} %get-tuple-element.120), channel_id=1, source_target_pairs={{0,20},{4,24},{8,28},{12,0},{16,4},{20,8},{24,12},{28,16},{1,21},{... | collective-permute-start | bytes 344072 | tf_op jit(solution)/shard_map/ppermute | solution.py:19
  402.7 17.6 %collective-permute-done.52.refs_5_ = bf16[224,640]{1,0:T(8,128)(2,1)S(1)} collective-permute-done((bf16[224,640]{1,0:T(8,128)(2,1)S(1)}, bf16[224,640]{1,0:T(8,128)(2,1)S(1)}, u32[]{:S(2)}, u32[]{:S(2)}) %collective-permute-start.52) | collective-permute-done | bytes 286752 | tf_op jit(solution)/shard_map/ppermute | solution.py:19
  (224 shorter events, 177.5 us)
Async XLA Ops:
  49.7 43.6 %collective-permute-start.21 = (bf16[2,256,384]{2,1,0:T(8,128)(2,1)S(1)}, bf16[2,256,384]{2,1,0:T(8,128)(2,1)S(1)}, u32[]{:S(2)}, u32[]{:S(2)}) collective-permute-start(bf16[2,256,384]{2,1,0:T(8,128)(2,1)S(1)} %add_convert_fusion), channel_id=1, source_target_pairs={{0,2},{1,3},{2,0},{3,1},{4,6},{5,7},{6,4},{7,5},{8,10},{9,11},{10,... | collective-permute-start | bytes 1179656 | tf_op jit(solution)/shard_map/ppermute | solution.py:19
  59.9 30.4 %collective-permute-start.5 = (bf16[2,256,256]{2,1,0:T(8,128)(2,1)S(1)}, bf16[2,256,256]{2,1,0:T(8,128)(2,1)S(1)}, u32[]{:S(2)}, u32[]{:S(2)}) collective-permute-start(bf16[2,256,256]{2,1,0:T(8,128)(2,1)S(1)} %pad_maximum_fusion.5.refs_4_), channel_id=1, source_target_pairs={{0,1},{1,0},{2,3},{3,2},{4,5},{5,4},{6,7},{7,6},{8,9},{9,8},{10,11... | collective-permute-start | bytes 786440 | tf_op jit(solution)/shard_map/ppermute | solution.py:32
  122.5 61.3 %collective-permute-start.58 = (bf16[2,256,512]{2,1,0:T(8,128)(2,1)S(1)}, bf16[2,256,512]{2,1,0:T(8,128)(2,1)S(1)}, u32[]{:S(2)}, u32[]{:S(2)}) collective-permute-start(bf16[2,256,512]{2,1,0:T(8,128)(2,1)S(1)} %pad_maximum_fusion.3.refs_4_), channel_id=1, source_target_pairs={{0,1},{1,0},{2,3},{3,2},{4,5},{5,4},{6,7},{7,6},{8,9},{9,8},{10,11... | collective-permute-start | bytes 1572872 | tf_op jit(solution)/shard_map/ppermute | solution.py:32
  143.5 89.7 %collective-permute-start.40 = (bf16[2,256,640]{2,1,0:T(8,128)(2,1)S(1)}, bf16[2,256,640]{2,1,0:T(8,128)(2,1)S(1)}, u32[]{:S(2)}, u32[]{:S(2)}) collective-permute-start(bf16[2,256,640]{2,1,0:T(8,128)(2,1)S(1)} %pad_maximum_fusion.1.refs_4_), channel_id=1, source_target_pairs={{0,1},{1,0},{2,3},{3,2},{4,5},{5,4},{6,7},{7,6},{8,9},{9,8},{10,11... | collective-permute-start | bytes 1966088 | tf_op jit(solution)/shard_map/ppermute | solution.py:32
  183.8 36.7 %collective-permute-start.33 = (bf16[224,384]{1,0:T(8,128)(2,1)S(1)}, bf16[224,384]{1,0:T(8,128)(2,1)S(1)}, u32[]{:S(2)}, u32[]{:S(2)}) collective-permute-start(bf16[224,384]{1,0:T(8,128)(2,1)S(1)} %get-tuple-element.139), channel_id=1, source_target_pairs={{0,16},{4,20},{8,24},{12,28},{16,0},{20,4},{24,8},{28,12},{1,17},{... | collective-permute-start | bytes 516104 | tf_op jit(solution)/shard_map/ppermute | solution.py:19
  188.1 45.1 %collective-permute-start.34 = (bf16[224,384]{1,0:T(8,128)(2,1)S(1)}, bf16[224,384]{1,0:T(8,128)(2,1)S(1)}, u32[]{:S(2)}, u32[]{:S(2)}) collective-permute-start(bf16[224,384]{1,0:T(8,128)(2,1)S(1)} %get-tuple-element.140), channel_id=1, source_target_pairs={{0,12},{4,16},{8,20},{12,24},{16,28},{20,0},{24,4},{28,8},{1,13},{... | collective-permute-start | bytes 516104 | tf_op jit(solution)/shard_map/ppermute | solution.py:19
  190.8 52.0 %collective-permute-start.59 = (bf16[224,512]{1,0:T(8,128)(2,1)S(1)}, bf16[224,512]{1,0:T(8,128)(2,1)S(1)}, u32[]{:S(2)}, u32[]{:S(2)}) collective-permute-start(bf16[224,512]{1,0:T(8,128)(2,1)S(1)} %get-tuple-element.172), channel_id=1, source_target_pairs={{0,4},{4,8},{8,12},{12,16},{16,20},{20,24},{24,28},{28,0},{1,5},{5... | collective-permute-start | bytes 688136 | tf_op jit(solution)/shard_map/ppermute | solution.py:19
  192.4 52.9 %collective-permute-start.60 = (bf16[224,512]{1,0:T(8,128)(2,1)S(1)}, bf16[224,512]{1,0:T(8,128)(2,1)S(1)}, u32[]{:S(2)}, u32[]{:S(2)}) collective-permute-start(bf16[224,512]{1,0:T(8,128)(2,1)S(1)} %get-tuple-element.173), channel_id=1, source_target_pairs={{0,8},{4,12},{8,16},{12,20},{16,24},{20,28},{24,0},{28,4},{1,9},{5... | collective-permute-start | bytes 688136 | tf_op jit(solution)/shard_map/ppermute | solution.py:19
  242.8 46.4 %collective-permute-start.41 = (bf16[224,640]{1,0:T(8,128)(2,1)S(1)}, bf16[224,640]{1,0:T(8,128)(2,1)S(1)}, u32[]{:S(2)}, u32[]{:S(2)}) collective-permute-start(bf16[224,640]{1,0:T(8,128)(2,1)S(1)} %get-tuple-element.150), channel_id=1, source_target_pairs={{0,4},{4,8},{8,12},{12,16},{16,20},{20,24},{24,28},{28,0},{1,5},{5... | collective-permute-start | bytes 860168 | tf_op jit(solution)/shard_map/ppermute | solution.py:19
  242.9 48.7 %collective-permute-start.42 = (bf16[224,640]{1,0:T(8,128)(2,1)S(1)}, bf16[224,640]{1,0:T(8,128)(2,1)S(1)}, u32[]{:S(2)}, u32[]{:S(2)}) collective-permute-start(bf16[224,640]{1,0:T(8,128)(2,1)S(1)} %get-tuple-element.151), channel_id=1, source_target_pairs={{0,8},{4,12},{8,16},{12,20},{16,24},{20,28},{24,0},{28,4},{1,9},{5... | collective-permute-start | bytes 860168 | tf_op jit(solution)/shard_map/ppermute | solution.py:19
  254.2 35.0 %collective-permute-start.65 = (bf16[224,512]{1,0:T(8,128)(2,1)S(1)}, bf16[224,512]{1,0:T(8,128)(2,1)S(1)}, u32[]{:S(2)}, u32[]{:S(2)}) collective-permute-start(bf16[224,512]{1,0:T(8,128)(2,1)S(1)} %get-tuple-element.178), channel_id=1, source_target_pairs={{0,28},{4,0},{8,4},{12,8},{16,12},{20,16},{24,20},{28,24},{1,29},{... | collective-permute-start | bytes 688136 | tf_op jit(solution)/shard_map/ppermute | solution.py:19
  259.7 35.1 %collective-permute-start.43 = (bf16[224,640]{1,0:T(8,128)(2,1)S(1)}, bf16[224,640]{1,0:T(8,128)(2,1)S(1)}, u32[]{:S(2)}, u32[]{:S(2)}) collective-permute-start(bf16[224,640]{1,0:T(8,128)(2,1)S(1)} %get-tuple-element.152), channel_id=1, source_target_pairs={{0,12},{4,16},{8,20},{12,24},{16,28},{20,0},{24,4},{28,8},{1,13},{... | collective-permute-start | bytes 860168 | tf_op jit(solution)/shard_map/ppermute | solution.py:19
  261.8 42.8 %collective-permute-start.44 = (bf16[224,640]{1,0:T(8,128)(2,1)S(1)}, bf16[224,640]{1,0:T(8,128)(2,1)S(1)}, u32[]{:S(2)}, u32[]{:S(2)}) collective-permute-start(bf16[224,640]{1,0:T(8,128)(2,1)S(1)} %get-tuple-element.153), channel_id=1, source_target_pairs={{0,16},{4,20},{8,24},{12,28},{16,0},{20,4},{24,8},{28,12},{1,17},{... | collective-permute-start | bytes 860168 | tf_op jit(solution)/shard_map/ppermute | solution.py:19
  289.2 31.7 %collective-permute-start.45 = (bf16[224,640]{1,0:T(8,128)(2,1)S(1)}, bf16[224,640]{1,0:T(8,128)(2,1)S(1)}, u32[]{:S(2)}, u32[]{:S(2)}) collective-permute-start(bf16[224,640]{1,0:T(8,128)(2,1)S(1)} %get-tuple-element.154), channel_id=1, source_target_pairs={{0,20},{4,24},{8,28},{12,0},{16,4},{20,8},{24,12},{28,16},{1,21},{... | collective-permute-start | bytes 860168 | tf_op jit(solution)/shard_map/ppermute | solution.py:19
  289.2 31.7 %collective-permute-start.46 = (bf16[224,640]{1,0:T(8,128)(2,1)S(1)}, bf16[224,640]{1,0:T(8,128)(2,1)S(1)}, u32[]{:S(2)}, u32[]{:S(2)}) collective-permute-start(bf16[224,640]{1,0:T(8,128)(2,1)S(1)} %get-tuple-element.155), channel_id=1, source_target_pairs={{0,24},{4,28},{8,0},{12,4},{16,8},{20,12},{24,16},{28,20},{1,25},{... | collective-permute-start | bytes 860168 | tf_op jit(solution)/shard_map/ppermute | solution.py:19
  294.8 41.5 %collective-permute-start.66 = (bf16[224,512]{1,0:T(8,128)(2,1)S(1)}, bf16[224,512]{1,0:T(8,128)(2,1)S(1)}, u32[]{:S(2)}, u32[]{:S(2)}) collective-permute-start(bf16[224,512]{1,0:T(8,128)(2,1)S(1)} %get-tuple-element.180), channel_id=1, source_target_pairs={{0,28},{4,0},{8,4},{12,8},{16,12},{20,16},{24,20},{28,24},{1,29},{... | collective-permute-start | bytes 688136 | tf_op jit(solution)/shard_map/ppermute | solution.py:19
  304.6 36.1 %collective-permute-start.67 = (bf16[224,512]{1,0:T(8,128)(2,1)S(1)}, bf16[224,512]{1,0:T(8,128)(2,1)S(1)}, u32[]{:S(2)}, u32[]{:S(2)}) collective-permute-start(bf16[224,512]{1,0:T(8,128)(2,1)S(1)} %get-tuple-element.181), channel_id=1, source_target_pairs={{0,24},{4,28},{8,0},{12,4},{16,8},{20,12},{24,16},{28,20},{1,25},{... | collective-permute-start | bytes 688136 | tf_op jit(solution)/shard_map/ppermute | solution.py:19
  336.3 41.9 %collective-permute-start.48 = (bf16[224,640]{1,0:T(8,128)(2,1)S(1)}, bf16[224,640]{1,0:T(8,128)(2,1)S(1)}, u32[]{:S(2)}, u32[]{:S(2)}) collective-permute-start(bf16[224,640]{1,0:T(8,128)(2,1)S(1)} %get-tuple-element.158), channel_id=1, source_target_pairs={{0,28},{4,0},{8,4},{12,8},{16,12},{20,16},{24,20},{28,24},{1,29},{... | collective-permute-start | bytes 860168 | tf_op jit(solution)/shard_map/ppermute | solution.py:19
  336.3 41.9 %collective-permute-start.49 = (bf16[224,640]{1,0:T(8,128)(2,1)S(1)}, bf16[224,640]{1,0:T(8,128)(2,1)S(1)}, u32[]{:S(2)}, u32[]{:S(2)}) collective-permute-start(bf16[224,640]{1,0:T(8,128)(2,1)S(1)} %get-tuple-element.159), channel_id=1, source_target_pairs={{0,24},{4,28},{8,0},{12,4},{16,8},{20,12},{24,16},{28,20},{1,25},{... | collective-permute-start | bytes 860168 | tf_op jit(solution)/shard_map/ppermute | solution.py:19
  367.7 35.0 %collective-permute-start.51 = (bf16[224,640]{1,0:T(8,128)(2,1)S(1)}, bf16[224,640]{1,0:T(8,128)(2,1)S(1)}, u32[]{:S(2)}, u32[]{:S(2)}) collective-permute-start(bf16[224,640]{1,0:T(8,128)(2,1)S(1)} %get-tuple-element.161), channel_id=1, source_target_pairs={{0,16},{4,20},{8,24},{12,28},{16,0},{20,4},{24,8},{28,12},{1,17},{... | collective-permute-start | bytes 860168 | tf_op jit(solution)/shard_map/ppermute | solution.py:19
  367.7 52.5 %collective-permute-start.52 = (bf16[224,640]{1,0:T(8,128)(2,1)S(1)}, bf16[224,640]{1,0:T(8,128)(2,1)S(1)}, u32[]{:S(2)}, u32[]{:S(2)}) collective-permute-start(bf16[224,640]{1,0:T(8,128)(2,1)S(1)} %get-tuple-element.162), channel_id=1, source_target_pairs={{0,12},{4,16},{8,20},{12,24},{16,28},{20,0},{24,4},{28,8},{1,13},{... | collective-permute-start | bytes 860168 | tf_op jit(solution)/shard_map/ppermute | solution.py:19
  378.3 42.0 %collective-permute-start.53 = (bf16[224,640]{1,0:T(8,128)(2,1)S(1)}, bf16[224,640]{1,0:T(8,128)(2,1)S(1)}, u32[]{:S(2)}, u32[]{:S(2)}) collective-permute-start(bf16[224,640]{1,0:T(8,128)(2,1)S(1)} %get-tuple-element.163), channel_id=1, source_target_pairs={{0,8},{4,12},{8,16},{12,20},{16,24},{20,28},{24,0},{28,4},{1,9},{5... | collective-permute-start | bytes 860168 | tf_op jit(solution)/shard_map/ppermute | solution.py:19
  378.3 42.0 %collective-permute-start.54 = (bf16[224,640]{1,0:T(8,128)(2,1)S(1)}, bf16[224,640]{1,0:T(8,128)(2,1)S(1)}, u32[]{:S(2)}, u32[]{:S(2)}) collective-permute-start(bf16[224,640]{1,0:T(8,128)(2,1)S(1)} %get-tuple-element.164), channel_id=1, source_target_pairs={{0,4},{4,8},{8,12},{12,16},{16,20},{20,24},{24,28},{28,0},{1,5},{5... | collective-permute-start | bytes 860168 | tf_op jit(solution)/shard_map/ppermute | solution.py:19
  381.7 43.6 %collective-permute-start.15 = (bf16[224,256]{1,0:T(8,128)(2,1)S(1)}, bf16[224,256]{1,0:T(8,128)(2,1)S(1)}, u32[]{:S(2)}, u32[]{:S(2)}) collective-permute-start(bf16[224,256]{1,0:T(8,128)(2,1)S(1)} %get-tuple-element.120), channel_id=1, source_target_pairs={{0,20},{4,24},{8,28},{12,0},{16,4},{20,8},{24,12},{28,16},{1,21},{... | collective-permute-start | bytes 344072 | tf_op jit(solution)/shard_map/ppermute | solution.py:19
  (72 other events, 965.4 us)

commit v2 on v1

--- a/solution.py
+++ b/solution.py
@@ -10,6 +10,7 @@
 
 learn_rate = 2.0
 AHEAD = 3
+LOADED = 2
 VMEM_LIMIT = 16 * 1024 * 1024
 CUTS = (2, 4, 5, 3, 2)
 
@@ -109,14 +110,18 @@
     )(*blocks, *held)
 
 
-def out_kernel(begin, scale, *refs):
-    weight_ref, own_ref, other_ref, part_ref, sem = refs[-5:]
-    chips = own_ref.shape[0]
-    hidden_refs, targets_refs = refs[: 2 * chips], refs[2 * chips : -5]
-    step = own_ref.shape[2]
-    copy = pltpu.make_async_copy(weight_ref.at[:, pl.ds(begin, step)], part_ref, sem)
-    copy.start()
-    copy.wait()
+def out_kernel(begin, scale, loaded, *refs):
+    if loaded:
+        part_ref, own_ref, other_ref = refs[-3:]
+        refs = refs[:-3]
+    else:
+        weight_ref, own_ref, other_ref, part_ref, sem = refs[-5:]
+        refs = refs[:-5]
+        copy = pltpu.make_async_copy(weight_ref.at[:, pl.ds(begin, own_ref.shape[2])], part_ref, sem)
+        copy.start()
+        copy.wait()
+    chips, _, step = own_ref.shape
+    hidden_refs, targets_refs = refs[: 2 * chips], refs[2 * chips :]
     for d in range(chips):
         own, other = (
             jnp.dot(ref[...], part_ref[...], preferred_element_type=jnp.float32) * scale
@@ -128,20 +133,24 @@
         other_ref[d] = other.astype(jnp.bfloat16)
 
 
-def out_part(hidden, targets, weight, begin, step, scale):
+def out_part(hidden, targets, weight, begin, step, scale, keep):
     chips, rows = len(hidden) // 2, hidden[0].shape[0]
     inside = pl.BlockSpec(memory_space=pltpu.VMEM)
     outside = pl.BlockSpec(memory_space=pl.ANY)
     units = weight.shape[0]
+    loaded = weight.shape[1] == step
     return pl.pallas_call(
-        functools.partial(out_kernel, begin, scale),
-        in_specs=[inside] * (2 * chips + len(targets)) + [outside],
-        out_specs=[inside, inside],
+        functools.partial(out_kernel, begin, scale, loaded),
+        in_specs=[inside] * (2 * chips + len(targets)) + [inside if loaded else outside],
+        out_specs=[inside] * (3 if keep else 2),
         out_shape=[
             jax.ShapeDtypeStruct((chips, rows, step), jnp.float32),
             jax.ShapeDtypeStruct((chips, rows, step), jnp.bfloat16),
-        ],
-        scratch_shapes=[pltpu.VMEM((units, step), jnp.bfloat16), pltpu.SemaphoreType.DMA],
+        ]
+        + ([jax.ShapeDtypeStruct((units, step), jnp.bfloat16)] if keep else []),
+        scratch_shapes=[]
+        if loaded
+        else ([] if keep else [pltpu.VMEM((units, step), jnp.bfloat16)]) + [pltpu.SemaphoreType.DMA],
         compiler_params=pltpu.CompilerParams(vmem_limit_bytes=VMEM_LIMIT),
         cost_estimate=pl.CostEstimate(
             flops=4 * chips * rows * units * step, bytes_accessed=2 * units * step, transcendentals=0
@@ -150,17 +159,22 @@
     )(*hidden, *targets, weight)
 
 
-def grad_kernel(begin, scale, chips, unrolled, *refs):
+def grad_kernel(begin, scale, chips, unrolled, loaded, *refs):
     hidden_refs, refs = refs[: 2 * chips], refs[2 * chips :]
     resid_ref, other_ref, weight_ref = refs[:3]
-    block_refs, (part_ref, stepped_ref, sem) = refs[3:-3], refs[-3:]
+    if loaded:
+        part_ref = weight_ref
+        block_refs, (stepped_ref,) = refs[3:-1], refs[-1:]
+    else:
+        block_refs, (stepped_ref, part_ref, sem) = refs[3:-3], refs[-3:]
     workers = len(block_refs)
     step = resid_ref.shape[2]
     units = part_ref.shape[0]
     block = units // workers
     tile = next(t for t in (256, 128) if units % t == 0)
-    copy = pltpu.make_async_copy(weight_ref.at[:, pl.ds(begin, step)], part_ref, sem)
-    copy.start()
+    if not loaded:
+        copy = pltpu.make_async_copy(weight_ref.at[:, pl.ds(begin, step)], part_ref, sem)
+        copy.start()
 
     def one_tile(i):
         at = pl.ds(i * tile if isinstance(i, int) else pl.multiple_of(i * tile, tile), tile)
@@ -173,7 +187,8 @@
                 preferred_element_type=jnp.float32,
             )
             grad = term if grad is None else grad + term
-        pl.when(i == 0)(copy.wait)
+        if not loaded:
+            pl.when(i == 0)(copy.wait)
         stepped_ref[at] = (part_ref[at].astype(jnp.float32) - scale * grad).astype(jnp.bfloat16)
 
     if unrolled:
@@ -190,18 +205,16 @@
 def grad_part(hidden, resid, other, weight, begin, scale, workers, unrolled):
     chips, rows, step = resid.shape
     units = weight.shape[0]
+    loaded = weight.shape[1] == step
     inside = pl.BlockSpec(memory_space=pltpu.VMEM)
     outside = pl.BlockSpec(memory_space=pl.ANY)
     return pl.pallas_call(
-        functools.partial(grad_kernel, begin, scale, chips, unrolled),
-        in_specs=[inside] * (2 * chips + 2) + [outside],
+        functools.partial(grad_kernel, begin, scale, chips, unrolled, loaded),
+        in_specs=[inside] * (2 * chips + 2) + [inside if loaded else outside],
         out_specs=[inside] * workers,
         out_shape=[jax.ShapeDtypeStruct((units // workers, step), jnp.bfloat16)] * workers,
-        scratch_shapes=[
-            pltpu.VMEM((units, step), jnp.bfloat16),
-            pltpu.VMEM((units, step), jnp.bfloat16),
-            pltpu.SemaphoreType.DMA,
-        ],
+        scratch_shapes=[pltpu.VMEM((units, step), jnp.bfloat16)]
+        + ([] if loaded else [pltpu.VMEM((units, step), jnp.bfloat16), pltpu.SemaphoreType.DMA]),
         compiler_params=pltpu.CompilerParams(vmem_limit_bytes=VMEM_LIMIT),
         cost_estimate=pl.CostEstimate(
             flops=4 * chips * rows * units * step, bytes_accessed=4 * units * step, transcendentals=0
@@ -236,18 +249,23 @@
     arrived = []
     for c in range(parts):
         step = unit * CUTS[c]
+        source = weight
         runs = ((0, 1), (1, chips)) if c < AHEAD and chips > 1 else ((0, chips),)
         sums = []
         got = {}
         for first, last in runs:
-            own, other = out_part(
+            keep = c < LOADED and source is weight
+            own, other, *part = out_part(
                 hidden[2 * first : 2 * last],
                 [] if first else [targets],
-                weight,
+                source,
                 begins[c],
                 step,
                 out_scale,
+                keep,
             )
+            if keep:
+                source = part[0]
             if sums:
                 own, *sums = lax.optimization_barrier((own, *sums))
             summed = (own + other_core(other).astype(jnp.float32)).astype(jnp.bfloat16)
@@ -265,7 +283,7 @@
                 totals[n] = totals[n] + x.astype(jnp.float32)
         resid = jnp.stack(totals).astype(jnp.bfloat16)
         other = other_core(resid)
-        blocks = grad_part(hidden, resid, other, weight, begins[c], learn_rate * out_scale, workers, c < 2)
+        blocks = grad_part(hidden, resid, other, source, begins[c], learn_rate * out_scale, workers, c < 2)
         arrived.append(exchanged(blocks, 1))
     returned = []
     for c in range(parts):

time: 429 us -> 426 us (level)
  starting transfers between devices: 205 us -> 185 us
  waiting for transfers between devices: 160 us -> 178 us
    ppermute x77, starting transfers between devices: 202 us -> 181 us  [shifted(): lax.ppermute(x, axis, [(i, (i + by) % devices) for i in range(devices)])]
    ppermute x77, waiting for transfers between devices: 160 us -> 178 us  [shifted(): lax.ppermute(x, axis, [(i, (i + by) % devices) for i in range(devices)])]
where the time goes in v2:
time: 426 us
  starting transfers between devices  185 us (43%)
  waiting for transfers between devices  178 us (42%)
  Pallas kernels  46.4 us (11%)
  matrix products  12.1 us (3%)
    ppermute x77, starting transfers between devices, shifted(): lax.ppermute(x, axis, [(i, (i + by) % devices) for i in range(devices)])  181 us
    ppermute x77, waiting for transfers between devices, shifted(): lax.ppermute(x, axis, [(i, (i + by) % devices) for i in range(devices)])  178 us
    pallas_call x5, Pallas kernels, grad_part(): pl.pallas_call(functools.partial(grad_kernel, begin, scale, chips, unroll...  15.8 us
    pallas_call x5, Pallas kernels, mix_blocks(): pl.pallas_call(functools.partial(mix_kernel, weights.shape[0], workers),...  13.1 us
    dot_general x4, matrix products, body(): jnp.dot(x, up_weight, preferred_element_type=jnp.float32)  12.1 us
    pallas_call x8, Pallas kernels, out_part(): pl.pallas_call(functools.partial(out_kernel, begin, scale, loaded), in_sp...  11.6 us
  transfers between devices with their start and end apart: 92, of which 28 were waited for; matrix products, arithmetic and copies ran while one was open for 4% of the time, Pallas kernels for 11%

profile of v2, /device:TPU:0, one launch (start us, length us, event | category | flops | bytes accessed | tf_op | source)
XLA Modules:
  0.0 425.6 jit_solution(12650490680560384503)
XLA Ops:
  4.4 5.7 %multiply_convert_fusion.3.refs_0_ = bf16[256,1792]{1,0:T(8,128)(2,1)S(1)} fusion(bf16[256,2048]{1,0:T(8,128)(2,1)} %param.5, bf16[2048,1792]{1,0:T(8,128)(2,1)} %param.7), kind=kOutput, calls=%fused_computation.4 | convolution fusion | flops 1881341952 | bytes 9306112 | tf_op jit(solution)/shard_map/dot_general | solution.py:242
  17.7 9.4 %collective-permute-done.1 = bf16[256,2048]{1,0:T(8,128)(2,1)S(1)} collective-permute-done((bf16[256,2048]{1,0:T(8,128)(2,1)}, bf16[256,2048]{1,0:T(8,128)(2,1)S(1)}, u32[]{:S(2)}, u32[]{:S(2)}) %collective-permute-start.1) | collective-permute-done | bytes 1048608 | tf_op jit(solution)/shard_map/ppermute | solution.py:20
  49.5 5.0 %collective-permute-done.4 = bf16[2,256,256]{2,1,0:T(8,128)(2,1)S(1)} collective-permute-done((bf16[2,256,256]{2,1,0:T(8,128)(2,1)S(1)}, bf16[2,256,256]{2,1,0:T(8,128)(2,1)S(1)}, u32[]{:S(2)}, u32[]{:S(2)}) %collective-permute-start.4) | collective-permute-done | bytes 262176 | tf_op jit(solution)/shard_map/ppermute | solution.py:20
  66.2 6.2 %collective-permute-done.80.refs_3_ = bf16[224,256]{1,0:T(8,128)(2,1)S(1)} collective-permute-done((bf16[224,256]{1,0:T(8,128)(2,1)S(1)}, bf16[224,256]{1,0:T(8,128)(2,1)S(1)}, u32[]{:S(2)}, u32[]{:S(2)}) %collective-permute-start.80) | collective-permute-done | bytes 114720 | tf_op jit(solution)/shard_map/ppermute | solution.py:20
  84.2 5.2 %collective-permute-start.85 = (bf16[224,256]{1,0:T(8,128)(2,1)S(1)}, bf16[224,256]{1,0:T(8,128)(2,1)S(1)}, u32[]{:S(2)}, u32[]{:S(2)}) collective-permute-start(bf16[224,256]{1,0:T(8,128)(2,1)S(1)} %get-tuple-element.206), channel_id=1, source_target_pairs={{0,28},{4,0},{8,4},{12,8},{16,12},{20,16},{24,20},{28,24},{1,29},{... | collective-permute-start | bytes 344072 | tf_op jit(solution)/shard_map/ppermute | solution.py:20
  92.9 7.5 %collective-permute-done.39 = bf16[2,256,640]{2,1,0:T(8,128)(2,1)S(1)} collective-permute-done((bf16[2,256,640]{2,1,0:T(8,128)(2,1)S(1)}, bf16[2,256,640]{2,1,0:T(8,128)(2,1)S(1)}, u32[]{:S(2)}, u32[]{:S(2)}) %collective-permute-start.39) | collective-permute-done | bytes 655392 | tf_op jit(solution)/shard_map/ppermute | solution.py:20
  122.2 8.2 %collective-permute-start.25 = (bf16[224,384]{1,0:T(8,128)(2,1)S(1)}, bf16[224,384]{1,0:T(8,128)(2,1)S(1)}, u32[]{:S(2)}, u32[]{:S(2)}) collective-permute-start(bf16[224,384]{1,0:T(8,128)(2,1)S(1)} %get-tuple-element.132), channel_id=1, source_target_pairs={{0,12},{4,16},{8,20},{12,24},{16,28},{20,0},{24,4},{28,8},{1,13},{... | collective-permute-start | bytes 516104 | tf_op jit(solution)/shard_map/ppermute | solution.py:20
  130.4 12.0 %collective-permute-done.8.refs_3_ = bf16[224,256]{1,0:T(8,128)(2,1)S(1)} collective-permute-done((bf16[224,256]{1,0:T(8,128)(2,1)S(1)}, bf16[224,256]{1,0:T(8,128)(2,1)S(1)}, u32[]{:S(2)}, u32[]{:S(2)}) %collective-permute-start.8) | collective-permute-done | bytes 114720 | tf_op jit(solution)/shard_map/ppermute | solution.py:20
  150.6 8.3 %collective-permute-start.29 = (bf16[224,384]{1,0:T(8,128)(2,1)S(1)}, bf16[224,384]{1,0:T(8,128)(2,1)S(1)}, u32[]{:S(2)}, u32[]{:S(2)}) collective-permute-start(bf16[224,384]{1,0:T(8,128)(2,1)S(1)} %get-tuple-element.136), channel_id=1, source_target_pairs={{0,28},{4,0},{8,4},{12,8},{16,12},{20,16},{24,20},{28,24},{1,29},{... | collective-permute-start | bytes 516104 | tf_op jit(solution)/shard_map/ppermute | solution.py:20
  191.1 12.9 %collective-permute-start.60 = (bf16[224,512]{1,0:T(8,128)(2,1)S(1)}, bf16[224,512]{1,0:T(8,128)(2,1)S(1)}, u32[]{:S(2)}, u32[]{:S(2)}) collective-permute-start(bf16[224,512]{1,0:T(8,128)(2,1)S(1)} %get-tuple-element.176), channel_id=1, source_target_pairs={{0,8},{4,12},{8,16},{12,20},{16,24},{20,28},{24,0},{28,4},{1,9},{5... | collective-permute-start | bytes 688136 | tf_op jit(solution)/shard_map/ppermute | solution.py:20
  204.0 15.6 %collective-permute-done.33.refs_4_ = bf16[224,384]{1,0:T(8,128)(2,1)S(1)} collective-permute-done((bf16[224,384]{1,0:T(8,128)(2,1)S(1)}, bf16[224,384]{1,0:T(8,128)(2,1)S(1)}, u32[]{:S(2)}, u32[]{:S(2)}) %collective-permute-start.33) | collective-permute-done | bytes 172064 | tf_op jit(solution)/shard_map/ppermute | solution.py:20
  219.6 10.8 %collective-permute-done.34.refs_5_ = bf16[224,384]{1,0:T(8,128)(2,1)S(1)} collective-permute-done((bf16[224,384]{1,0:T(8,128)(2,1)S(1)}, bf16[224,384]{1,0:T(8,128)(2,1)S(1)}, u32[]{:S(2)}, u32[]{:S(2)}) %collective-permute-start.34) | collective-permute-done | bytes 172064 | tf_op jit(solution)/shard_map/ppermute | solution.py:20
  230.5 5.4 %grad_part.7 = (bf16[224,640]{1,0:T(8,128)(2,1)S(1)}, bf16[224,640]{1,0:T(8,128)(2,1)S(1)}, bf16[224,640]{1,0:T(8,128)(2,1)S(1)}, bf16[224,640]{1,0:T(8,128)(2,1...) custom-call(bf16[256,1792]{1,0:T(8,128)(2,1)S(1)} %multiply_convert_, ...), custom_call_target="tpu_custom_call" | custom-call | flops 2348810240 | bytes 4587520 | tf_op jit(solution)/shard_map/grad_part/pallas_call | solution.py:211
  240.2 7.3 %collective-permute-start.42 = (bf16[224,640]{1,0:T(8,128)(2,1)S(1)}, bf16[224,640]{1,0:T(8,128)(2,1)S(1)}, u32[]{:S(2)}, u32[]{:S(2)}) collective-permute-start(bf16[224,640]{1,0:T(8,128)(2,1)S(1)} %get-tuple-element.153), channel_id=1, source_target_pairs={{0,8},{4,12},{8,16},{12,20},{16,24},{20,28},{24,0},{28,4},{1,9},{5... | collective-permute-start | bytes 860168 | tf_op jit(solution)/shard_map/ppermute | solution.py:20
  247.6 5.8 %collective-permute-start.64 = (bf16[224,512]{1,0:T(8,128)(2,1)S(1)}, bf16[224,512]{1,0:T(8,128)(2,1)S(1)}, u32[]{:S(2)}, u32[]{:S(2)}) collective-permute-start(bf16[224,512]{1,0:T(8,128)(2,1)S(1)} %get-tuple-element.180), channel_id=1, source_target_pairs={{0,24},{4,28},{8,0},{12,4},{16,8},{20,12},{24,16},{28,20},{1,25},{... | collective-permute-start | bytes 688136 | tf_op jit(solution)/shard_map/ppermute | solution.py:20
  253.9 5.2 %collective-permute-done.63.refs_5_ = bf16[224,512]{1,0:T(8,128)(2,1)S(1)} collective-permute-done((bf16[224,512]{1,0:T(8,128)(2,1)S(1)}, bf16[224,512]{1,0:T(8,128)(2,1)S(1)}, u32[]{:S(2)}, u32[]{:S(2)}) %collective-permute-start.63) | collective-permute-done | bytes 229408 | tf_op jit(solution)/shard_map/ppermute | solution.py:20
  259.9 28.7 %collective-permute-start.44 = (bf16[224,640]{1,0:T(8,128)(2,1)S(1)}, bf16[224,640]{1,0:T(8,128)(2,1)S(1)}, u32[]{:S(2)}, u32[]{:S(2)}) collective-permute-start(bf16[224,640]{1,0:T(8,128)(2,1)S(1)} %get-tuple-element.155), channel_id=1, source_target_pairs={{0,16},{4,20},{8,24},{12,28},{16,0},{20,4},{24,8},{28,12},{1,17},{... | collective-permute-start | bytes 860168 | tf_op jit(solution)/shard_map/ppermute | solution.py:20
  297.6 6.3 %collective-permute-done.44.refs_4_ = bf16[224,640]{1,0:T(8,128)(2,1)S(1)} collective-permute-done((bf16[224,640]{1,0:T(8,128)(2,1)S(1)}, bf16[224,640]{1,0:T(8,128)(2,1)S(1)}, u32[]{:S(2)}, u32[]{:S(2)}) %collective-permute-start.44) | collective-permute-done | bytes 286752 | tf_op jit(solution)/shard_map/ppermute | solution.py:20
  303.9 15.0 %collective-permute-start.67 = (bf16[224,512]{1,0:T(8,128)(2,1)S(1)}, bf16[224,512]{1,0:T(8,128)(2,1)S(1)}, u32[]{:S(2)}, u32[]{:S(2)}) collective-permute-start(bf16[224,512]{1,0:T(8,128)(2,1)S(1)} %get-tuple-element.184), channel_id=1, source_target_pairs={{0,24},{4,28},{8,0},{12,4},{16,8},{20,12},{24,16},{28,20},{1,25},{... | collective-permute-start | bytes 688136 | tf_op jit(solution)/shard_map/ppermute | solution.py:20
  319.0 10.5 %collective-permute-start.36 = (bf16[224,384]{1,0:T(8,128)(2,1)S(1)}, bf16[224,384]{1,0:T(8,128)(2,1)S(1)}, u32[]{:S(2)}, u32[]{:S(2)}) collective-permute-start(bf16[224,384]{1,0:T(8,128)(2,1)S(1)} %get-tuple-element.144), channel_id=1, source_target_pairs={{0,4},{4,8},{8,12},{12,16},{16,20},{20,24},{24,28},{28,0},{1,5},{5... | collective-permute-start | bytes 516104 | tf_op jit(solution)/shard_map/ppermute | solution.py:20
  333.2 23.0 %collective-permute-done.36.refs_7_ = bf16[224,384]{1,0:T(8,128)(2,1)S(1)} collective-permute-done((bf16[224,384]{1,0:T(8,128)(2,1)S(1)}, bf16[224,384]{1,0:T(8,128)(2,1)S(1)}, u32[]{:S(2)}, u32[]{:S(2)}) %collective-permute-start.36) | collective-permute-done | bytes 172064 | tf_op jit(solution)/shard_map/ppermute | solution.py:20
  361.4 25.7 %collective-permute-done.70.refs_5_ = bf16[224,512]{1,0:T(8,128)(2,1)S(1)} collective-permute-done((bf16[224,512]{1,0:T(8,128)(2,1)S(1)}, bf16[224,512]{1,0:T(8,128)(2,1)S(1)}, u32[]{:S(2)}, u32[]{:S(2)}) %collective-permute-start.70) | collective-permute-done | bytes 229408 | tf_op jit(solution)/shard_map/ppermute | solution.py:20
  396.6 10.9 %collective-permute-start.15 = (bf16[224,256]{1,0:T(8,128)(2,1)S(1)}, bf16[224,256]{1,0:T(8,128)(2,1)S(1)}, u32[]{:S(2)}, u32[]{:S(2)}) collective-permute-start(bf16[224,256]{1,0:T(8,128)(2,1)S(1)} %get-tuple-element.122), channel_id=1, source_target_pairs={{0,20},{4,24},{8,28},{12,0},{16,4},{20,8},{24,12},{28,16},{1,21},{... | collective-permute-start | bytes 344072 | tf_op jit(solution)/shard_map/ppermute | solution.py:20
  407.6 9.0 %collective-permute-done.52.refs_5_ = bf16[224,640]{1,0:T(8,128)(2,1)S(1)} collective-permute-done((bf16[224,640]{1,0:T(8,128)(2,1)S(1)}, bf16[224,640]{1,0:T(8,128)(2,1)S(1)}, u32[]{:S(2)}, u32[]{:S(2)}) %collective-permute-start.52) | collective-permute-done | bytes 286752 | tf_op jit(solution)/shard_map/ppermute | solution.py:20
  (224 shorter events, 165.0 us)
Async XLA Ops:
  49.2 43.2 %collective-permute-start.21 = (bf16[2,256,384]{2,1,0:T(8,128)(2,1)S(1)}, bf16[2,256,384]{2,1,0:T(8,128)(2,1)S(1)}, u32[]{:S(2)}, u32[]{:S(2)}) collective-permute-start(bf16[2,256,384]{2,1,0:T(8,128)(2,1)S(1)} %add_convert_fusion), channel_id=1, source_target_pairs={{0,2},{1,3},{2,0},{3,1},{4,6},{5,7},{6,4},{7,5},{8,10},{9,11},{10,... | collective-permute-start | bytes 1179656 | tf_op jit(solution)/shard_map/ppermute | solution.py:20
  59.0 30.4 %collective-permute-start.5 = (bf16[2,256,256]{2,1,0:T(8,128)(2,1)S(1)}, bf16[2,256,256]{2,1,0:T(8,128)(2,1)S(1)}, u32[]{:S(2)}, u32[]{:S(2)}) collective-permute-start(bf16[2,256,256]{2,1,0:T(8,128)(2,1)S(1)} %pad_maximum_fusion.5.refs_4_), channel_id=1, source_target_pairs={{0,1},{1,0},{2,3},{3,2},{4,5},{5,4},{6,7},{7,6},{8,9},{9,8},{10,11... | collective-permute-start | bytes 786440 | tf_op jit(solution)/shard_map/ppermute | solution.py:33
  121.6 61.3 %collective-permute-start.58 = (bf16[2,256,512]{2,1,0:T(8,128)(2,1)S(1)}, bf16[2,256,512]{2,1,0:T(8,128)(2,1)S(1)}, u32[]{:S(2)}, u32[]{:S(2)}) collective-permute-start(bf16[2,256,512]{2,1,0:T(8,128)(2,1)S(1)} %pad_maximum_fusion.3.refs_4_), channel_id=1, source_target_pairs={{0,1},{1,0},{2,3},{3,2},{4,5},{5,4},{6,7},{7,6},{8,9},{9,8},{10,11... | collective-permute-start | bytes 1572872 | tf_op jit(solution)/shard_map/ppermute | solution.py:33
  142.5 88.0 %collective-permute-start.40 = (bf16[2,256,640]{2,1,0:T(8,128)(2,1)S(1)}, bf16[2,256,640]{2,1,0:T(8,128)(2,1)S(1)}, u32[]{:S(2)}, u32[]{:S(2)}) collective-permute-start(bf16[2,256,640]{2,1,0:T(8,128)(2,1)S(1)} %pad_maximum_fusion.1.refs_4_), channel_id=1, source_target_pairs={{0,1},{1,0},{2,3},{3,2},{4,5},{5,4},{6,7},{7,6},{8,9},{9,8},{10,11... | collective-permute-start | bytes 1966088 | tf_op jit(solution)/shard_map/ppermute | solution.py:33
  182.9 36.7 %collective-permute-start.33 = (bf16[224,384]{1,0:T(8,128)(2,1)S(1)}, bf16[224,384]{1,0:T(8,128)(2,1)S(1)}, u32[]{:S(2)}, u32[]{:S(2)}) collective-permute-start(bf16[224,384]{1,0:T(8,128)(2,1)S(1)} %get-tuple-element.141), channel_id=1, source_target_pairs={{0,16},{4,20},{8,24},{12,28},{16,0},{20,4},{24,8},{28,12},{1,17},{... | collective-permute-start | bytes 516104 | tf_op jit(solution)/shard_map/ppermute | solution.py:20
  187.0 43.4 %collective-permute-start.34 = (bf16[224,384]{1,0:T(8,128)(2,1)S(1)}, bf16[224,384]{1,0:T(8,128)(2,1)S(1)}, u32[]{:S(2)}, u32[]{:S(2)}) collective-permute-start(bf16[224,384]{1,0:T(8,128)(2,1)S(1)} %get-tuple-element.142), channel_id=1, source_target_pairs={{0,12},{4,16},{8,20},{12,24},{16,28},{20,0},{24,4},{28,8},{1,13},{... | collective-permute-start | bytes 516104 | tf_op jit(solution)/shard_map/ppermute | solution.py:20
  189.3 50.9 %collective-permute-start.59 = (bf16[224,512]{1,0:T(8,128)(2,1)S(1)}, bf16[224,512]{1,0:T(8,128)(2,1)S(1)}, u32[]{:S(2)}, u32[]{:S(2)}) collective-permute-start(bf16[224,512]{1,0:T(8,128)(2,1)S(1)} %get-tuple-element.175), channel_id=1, source_target_pairs={{0,4},{4,8},{8,12},{12,16},{16,20},{20,24},{24,28},{28,0},{1,5},{5... | collective-permute-start | bytes 688136 | tf_op jit(solution)/shard_map/ppermute | solution.py:20
  191.1 56.4 %collective-permute-start.60 = (bf16[224,512]{1,0:T(8,128)(2,1)S(1)}, bf16[224,512]{1,0:T(8,128)(2,1)S(1)}, u32[]{:S(2)}, u32[]{:S(2)}) collective-permute-start(bf16[224,512]{1,0:T(8,128)(2,1)S(1)} %get-tuple-element.176), channel_id=1, source_target_pairs={{0,8},{4,12},{8,16},{12,20},{16,24},{20,28},{24,0},{28,4},{1,9},{5... | collective-permute-start | bytes 688136 | tf_op jit(solution)/shard_map/ppermute | solution.py:20
  240.2 48.4 %collective-permute-start.41 = (bf16[224,640]{1,0:T(8,128)(2,1)S(1)}, bf16[224,640]{1,0:T(8,128)(2,1)S(1)}, u32[]{:S(2)}, u32[]{:S(2)}) collective-permute-start(bf16[224,640]{1,0:T(8,128)(2,1)S(1)} %get-tuple-element.152), channel_id=1, source_target_pairs={{0,4},{4,8},{8,12},{12,16},{16,20},{20,24},{24,28},{28,0},{1,5},{5... | collective-permute-start | bytes 860168 | tf_op jit(solution)/shard_map/ppermute | solution.py:20
  240.2 50.7 %collective-permute-start.42 = (bf16[224,640]{1,0:T(8,128)(2,1)S(1)}, bf16[224,640]{1,0:T(8,128)(2,1)S(1)}, u32[]{:S(2)}, u32[]{:S(2)}) collective-permute-start(bf16[224,640]{1,0:T(8,128)(2,1)S(1)} %get-tuple-element.153), channel_id=1, source_target_pairs={{0,8},{4,12},{8,16},{12,20},{16,24},{20,28},{24,0},{28,4},{1,9},{5... | collective-permute-start | bytes 860168 | tf_op jit(solution)/shard_map/ppermute | solution.py:20
  253.4 35.2 %collective-permute-start.65 = (bf16[224,512]{1,0:T(8,128)(2,1)S(1)}, bf16[224,512]{1,0:T(8,128)(2,1)S(1)}, u32[]{:S(2)}, u32[]{:S(2)}) collective-permute-start(bf16[224,512]{1,0:T(8,128)(2,1)S(1)} %get-tuple-element.181), channel_id=1, source_target_pairs={{0,28},{4,0},{8,4},{12,8},{16,12},{20,16},{24,20},{28,24},{1,29},{... | collective-permute-start | bytes 688136 | tf_op jit(solution)/shard_map/ppermute | solution.py:20
  259.1 35.1 %collective-permute-start.43 = (bf16[224,640]{1,0:T(8,128)(2,1)S(1)}, bf16[224,640]{1,0:T(8,128)(2,1)S(1)}, u32[]{:S(2)}, u32[]{:S(2)}) collective-permute-start(bf16[224,640]{1,0:T(8,128)(2,1)S(1)} %get-tuple-element.154), channel_id=1, source_target_pairs={{0,12},{4,16},{8,20},{12,24},{16,28},{20,0},{24,4},{28,8},{1,13},{... | collective-permute-start | bytes 860168 | tf_op jit(solution)/shard_map/ppermute | solution.py:20
  259.9 44.0 %collective-permute-start.44 = (bf16[224,640]{1,0:T(8,128)(2,1)S(1)}, bf16[224,640]{1,0:T(8,128)(2,1)S(1)}, u32[]{:S(2)}, u32[]{:S(2)}) collective-permute-start(bf16[224,640]{1,0:T(8,128)(2,1)S(1)} %get-tuple-element.155), channel_id=1, source_target_pairs={{0,16},{4,20},{8,24},{12,28},{16,0},{20,4},{24,8},{28,12},{1,17},{... | collective-permute-start | bytes 860168 | tf_op jit(solution)/shard_map/ppermute | solution.py:20
  288.6 30.4 %collective-permute-start.45 = (bf16[224,640]{1,0:T(8,128)(2,1)S(1)}, bf16[224,640]{1,0:T(8,128)(2,1)S(1)}, u32[]{:S(2)}, u32[]{:S(2)}) collective-permute-start(bf16[224,640]{1,0:T(8,128)(2,1)S(1)} %get-tuple-element.156), channel_id=1, source_target_pairs={{0,20},{4,24},{8,28},{12,0},{16,4},{20,8},{24,12},{28,16},{1,21},{... | collective-permute-start | bytes 860168 | tf_op jit(solution)/shard_map/ppermute | solution.py:20
  288.6 30.4 %collective-permute-start.46 = (bf16[224,640]{1,0:T(8,128)(2,1)S(1)}, bf16[224,640]{1,0:T(8,128)(2,1)S(1)}, u32[]{:S(2)}, u32[]{:S(2)}) collective-permute-start(bf16[224,640]{1,0:T(8,128)(2,1)S(1)} %get-tuple-element.157), channel_id=1, source_target_pairs={{0,24},{4,28},{8,0},{12,4},{16,8},{20,12},{24,16},{28,20},{1,25},{... | collective-permute-start | bytes 860168 | tf_op jit(solution)/shard_map/ppermute | solution.py:20
  294.2 62.0 %collective-permute-start.66 = (bf16[224,512]{1,0:T(8,128)(2,1)S(1)}, bf16[224,512]{1,0:T(8,128)(2,1)S(1)}, u32[]{:S(2)}, u32[]{:S(2)}) collective-permute-start(bf16[224,512]{1,0:T(8,128)(2,1)S(1)} %get-tuple-element.183), channel_id=1, source_target_pairs={{0,28},{4,0},{8,4},{12,8},{16,12},{20,16},{24,20},{28,24},{1,29},{... | collective-permute-start | bytes 688136 | tf_op jit(solution)/shard_map/ppermute | solution.py:20
  303.9 52.3 %collective-permute-start.67 = (bf16[224,512]{1,0:T(8,128)(2,1)S(1)}, bf16[224,512]{1,0:T(8,128)(2,1)S(1)}, u32[]{:S(2)}, u32[]{:S(2)}) collective-permute-start(bf16[224,512]{1,0:T(8,128)(2,1)S(1)} %get-tuple-element.184), channel_id=1, source_target_pairs={{0,24},{4,28},{8,0},{12,4},{16,8},{20,12},{24,16},{28,20},{1,25},{... | collective-permute-start | bytes 688136 | tf_op jit(solution)/shard_map/ppermute | solution.py:20
  318.9 40.8 %collective-permute-start.68 = (bf16[224,512]{1,0:T(8,128)(2,1)S(1)}, bf16[224,512]{1,0:T(8,128)(2,1)S(1)}, u32[]{:S(2)}, u32[]{:S(2)}) collective-permute-start(bf16[224,512]{1,0:T(8,128)(2,1)S(1)} %get-tuple-element.185), channel_id=1, source_target_pairs={{0,20},{4,24},{8,28},{12,0},{16,4},{20,8},{24,12},{28,16},{1,21},{... | collective-permute-start | bytes 688136 | tf_op jit(solution)/shard_map/ppermute | solution.py:20
  319.0 41.1 %collective-permute-start.69 = (bf16[224,512]{1,0:T(8,128)(2,1)S(1)}, bf16[224,512]{1,0:T(8,128)(2,1)S(1)}, u32[]{:S(2)}, u32[]{:S(2)}) collective-permute-start(bf16[224,512]{1,0:T(8,128)(2,1)S(1)} %get-tuple-element.186), channel_id=1, source_target_pairs={{0,16},{4,20},{8,24},{12,28},{16,0},{20,4},{24,8},{28,12},{1,17},{... | collective-permute-start | bytes 688136 | tf_op jit(solution)/shard_map/ppermute | solution.py:20
  319.0 37.2 %collective-permute-start.36 = (bf16[224,384]{1,0:T(8,128)(2,1)S(1)}, bf16[224,384]{1,0:T(8,128)(2,1)S(1)}, u32[]{:S(2)}, u32[]{:S(2)}) collective-permute-start(bf16[224,384]{1,0:T(8,128)(2,1)S(1)} %get-tuple-element.144), channel_id=1, source_target_pairs={{0,4},{4,8},{8,12},{12,16},{16,20},{20,24},{24,28},{28,0},{1,5},{5... | collective-permute-start | bytes 516104 | tf_op jit(solution)/shard_map/ppermute | solution.py:20
  356.2 34.0 %collective-permute-start.48 = (bf16[224,640]{1,0:T(8,128)(2,1)S(1)}, bf16[224,640]{1,0:T(8,128)(2,1)S(1)}, u32[]{:S(2)}, u32[]{:S(2)}) collective-permute-start(bf16[224,640]{1,0:T(8,128)(2,1)S(1)} %get-tuple-element.160), channel_id=1, source_target_pairs={{0,28},{4,0},{8,4},{12,8},{16,12},{20,16},{24,20},{28,24},{1,29},{... | collective-permute-start | bytes 860168 | tf_op jit(solution)/shard_map/ppermute | solution.py:20
  356.2 34.0 %collective-permute-start.49 = (bf16[224,640]{1,0:T(8,128)(2,1)S(1)}, bf16[224,640]{1,0:T(8,128)(2,1)S(1)}, u32[]{:S(2)}, u32[]{:S(2)}) collective-permute-start(bf16[224,640]{1,0:T(8,128)(2,1)S(1)} %get-tuple-element.161), channel_id=1, source_target_pairs={{0,24},{4,28},{8,0},{12,4},{16,8},{20,12},{24,16},{28,20},{1,25},{... | collective-permute-start | bytes 860168 | tf_op jit(solution)/shard_map/ppermute | solution.py:20
  356.2 30.9 %collective-permute-start.70 = (bf16[224,512]{1,0:T(8,128)(2,1)S(1)}, bf16[224,512]{1,0:T(8,128)(2,1)S(1)}, u32[]{:S(2)}, u32[]{:S(2)}) collective-permute-start(bf16[224,512]{1,0:T(8,128)(2,1)S(1)} %get-tuple-element.187), channel_id=1, source_target_pairs={{0,12},{4,16},{8,20},{12,24},{16,28},{20,0},{24,4},{28,8},{1,13},{... | collective-permute-start | bytes 688136 | tf_op jit(solution)/shard_map/ppermute | solution.py:20
  387.2 29.4 %collective-permute-start.52 = (bf16[224,640]{1,0:T(8,128)(2,1)S(1)}, bf16[224,640]{1,0:T(8,128)(2,1)S(1)}, u32[]{:S(2)}, u32[]{:S(2)}) collective-permute-start(bf16[224,640]{1,0:T(8,128)(2,1)S(1)} %get-tuple-element.164), channel_id=1, source_target_pairs={{0,12},{4,16},{8,20},{12,24},{16,28},{20,0},{24,4},{28,8},{1,13},{... | collective-permute-start | bytes 860168 | tf_op jit(solution)/shard_map/ppermute | solution.py:20
  (72 other events, 963.4 us)
